TPU v7x, 256 devices: a whole 4x4x8 slice. The times are simulated.
256 devices in a mesh: ctx: 32 (over y, z_lo, core), section: 8 (over z_hi, x).
Axes of the slice: x: 4, y: 4, z: 8 (z_hi: 2, z_lo: 4; z = z_hi * 4 + z_lo), core: 2. Of those that a mesh axis runs over, the one named last changes fastest.
Arguments:
- queries: bfloat16 [8, 4096, 2560], P('section', 'ctx'), may hold values from -80 to 80
- grad_out: bfloat16 [8, 4096, 2560], P('section', 'ctx'), may hold values from -6 to 6
- keys_values: bfloat16 [2, 4096, 512], P(None, 'ctx'), may hold values from -16 to 16
- doc_ids: int32 [4096], replicated, may hold values from 0 to 7, never falling along the last dimension, each value on 1 to 1024 neighbouring positions
Outputs:
- grad_queries: bfloat16 [8, 4096, 2560], P('section', 'ctx')
- grad_kv: bfloat16 [2, 4096, 512], P(None, ('ctx', 'section'))
Inputs may be any that keep to these rules, and one draw needn't show every extreme that they name: `doc_ids`: document numbers never fall along the sequence; a document has at most 1024 tokens.
All inputs are finite; a program needn't handle non-finite values.
Results may differ from a plain program's by a relative error of at most 0.015.
Values may be sent and summed in bfloat16 or wider, within the bound.
No kernel may reach another device: no remote copies, remote signals or barrier semaphores. Data moves between devices by JAX's collectives and lax.ppermute only.
A program may use at most 64 MiB of HBM per device.

v0:
```python
import jax
import jax.numpy as jnp
from jax import lax
from jax.sharding import PartitionSpec as P

HD = 128


def from_behind(value, axis, steps):
    count = lax.axis_size(axis)
    first, last = (max(0, -steps), min(count, count - steps))
    return lax.ppermute(value, axis, [(source, source + steps) for source in range(first, last)])


def split_up(value, dim, length):
    before, after = (value.shape[:dim], value.shape[dim + 1 :])
    return jnp.moveaxis(value.reshape(*before, length, -1, *after), dim, 0)


def summed_on_arrival(value, axis, dim):
    blocks = split_up(value, dim, lax.axis_size(axis))
    arrived = lax.all_to_all(blocks, axis, split_axis=0, concat_axis=0, tiled=True)
    return arrived.astype(jnp.float32).sum(axis=0)


def body(queries, grad_out, keys_values, doc_ids):
    layers, tok_rows, width = queries.shape
    kv_width = keys_values.shape[2]
    heads_kv = kv_width // HD
    group = width // kv_width
    scale = HD ** (-0.5)
    reach = lax.axis_size("ctx") // 4
    span = reach + 1
    pieces = [keys_values]
    for offset in range(1, reach + 1):
        pieces.append(from_behind(keys_values, "ctx", offset))
    whole = jnp.concatenate(pieces[::-1], axis=1)
    total = span * tok_rows
    keys = whole[0].reshape(total, heads_kv, HD)
    values = whole[1].reshape(total, heads_kv, HD)
    qrows = queries.reshape(layers, tok_rows, heads_kv, group, HD)
    grows = grad_out.reshape(layers, tok_rows, heads_kv, group, HD)
    first = lax.axis_index("ctx") * tok_rows
    qplace = first + jnp.arange(tok_rows, dtype=jnp.int32)
    qdoc = lax.dynamic_slice_in_dim(doc_ids, first, tok_rows, 0)
    padded_docs = jnp.concatenate([jnp.full((reach * tok_rows,), -1, jnp.int32), doc_ids])
    window_docs = lax.dynamic_slice_in_dim(padded_docs, first, total, 0)
    window_places = first - reach * tok_rows + jnp.arange(total, dtype=jnp.int32)
    shards = 1
    for count in range(1, span + 1):
        if span % count == 0 and count * tok_rows <= max(512, tok_rows):
            shards = count
    kblock = shards * tok_rows
    nblocks = span // shards

    def block_parts(index):
        start = index * kblock
        kplace = lax.dynamic_slice_in_dim(window_places, start, kblock, 0)
        kdoc = lax.dynamic_slice_in_dim(window_docs, start, kblock, 0)
        visible = (kplace[None, :] <= qplace[:, None]) & (kdoc[None, :] == qdoc[:, None])
        kpart = lax.dynamic_slice_in_dim(keys, start, kblock, 0)
        vpart = lax.dynamic_slice_in_dim(values, start, kblock, 0)
        return (visible, kpart, vpart)

    def block_scores(kpart, visible):
        scores = (
            jnp.einsum("ltgnd,kgd->ltgnk", qrows, kpart, preferred_element_type=jnp.float32) * scale
        )
        return jnp.where(visible[None, :, None, None, :], scores, -1e30)

    def forward_step(carry, index):
        visible, kpart, vpart = block_parts(index)
        top, summed, accum = carry
        seen = visible[None, :, None, None, :]
        scores = block_scores(kpart, visible)
        new_top = jnp.maximum(top, jnp.max(scores, axis=-1))
        factor = jnp.exp(top - new_top)
        weights = jnp.where(seen, jnp.exp(scores - new_top[..., None]), 0.0)
        summed = summed * factor + jnp.sum(weights, axis=-1)
        accum = accum * factor[..., None] + jnp.einsum(
            "ltgnk,kgd->ltgnd", weights, vpart.astype(jnp.float32)
        )
        carry = (new_top, summed, accum)
        return (carry, None)

    stat_shape = (layers, tok_rows, heads_kv, group)
    start_state = (
        jnp.full(stat_shape, -1e30, jnp.float32),
        jnp.zeros(stat_shape, jnp.float32),
        jnp.zeros(stat_shape + (HD,), jnp.float32),
    )
    (top, summed, accum), unused = lax.scan(
        forward_step, start_state, jnp.arange(nblocks, dtype=jnp.int32)
    )
    lse = top + jnp.log(summed)
    delta = jnp.sum(grows.astype(jnp.float32) * (accum / summed[..., None]), axis=-1)

    def backward_step(dquery, index):
        visible, kpart, vpart = block_parts(index)
        backward_dquery = dquery
        seen = visible[None, :, None, None, :]
        scores = block_scores(kpart, visible)
        prob = jnp.where(seen, jnp.exp(scores - lse[..., None]), 0.0).astype(jnp.bfloat16)
        dprob = jnp.einsum("ltgnd,kgd->ltgnk", grows, vpart, preferred_element_type=jnp.float32)
        dscore = (prob.astype(jnp.float32) * (dprob - delta[..., None])).astype(jnp.bfloat16)
        backward_dquery = backward_dquery + scale * jnp.einsum(
            "ltgnk,kgd->ltgnd", dscore, kpart, preferred_element_type=jnp.float32
        )
        dkeys = scale * jnp.einsum(
            "ltgnk,ltgnd->kgd", dscore, qrows, preferred_element_type=jnp.float32
        )
        dvalues = jnp.einsum("ltgnk,ltgnd->kgd", prob, grows, preferred_element_type=jnp.float32)
        return (backward_dquery, (dkeys, dvalues))

    dquery, (dkeys, dvalues) = lax.scan(
        backward_step,
        jnp.zeros(stat_shape + (HD,), jnp.float32),
        jnp.arange(nblocks, dtype=jnp.int32),
    )
    grad_queries = dquery.reshape(layers, tok_rows, width).astype(jnp.bfloat16)
    grads = jnp.stack([dkeys.reshape(total, kv_width), dvalues.reshape(total, kv_width)]).reshape(
        2, span, tok_rows, kv_width
    )
    collected = grads[:, reach]
    for offset in range(1, reach + 1):
        collected = collected + from_behind(
            grads[:, reach - offset].astype(jnp.bfloat16), "ctx", -offset
        ).astype(jnp.float32)
    gathered = summed_on_arrival(collected.astype(jnp.bfloat16), "section", 1)
    grad_kv = gathered.astype(jnp.bfloat16)
    return (grad_queries, grad_kv)


def solution(mesh):
    return jax.shard_map(
        body,
        mesh=mesh,
        in_specs=(P("section", "ctx", None), P("section", "ctx", None), P(None, "ctx", None), P()),
        out_specs=(P("section", "ctx", None), P(None, ("ctx", "section"), None)),
        check_vma=False,
    )
```

profile of v0, /device:TPU:105, one launch (start us, length us, event | category | flops | bytes accessed | tf_op | source)
XLA Modules:
  0.0 208.0 jit_solution(15155738019538326137)
XLA Ops:
  1.8 3.2 %collective-permute-start = (bf16[2,128,512]{1,2,0:T(8,128)(2,1)S(1)}, bf16[2,128,512]{1,2,0:T(8,128)(2,1)}, u32[]{:S(2)}, u32[]{:S(2)}) collective-permute-start(bf16[2,128,512]{1,2,0:T(8,128)(2,1)S(1)} %copy.54), channel_id=1, source_target_pairs={{0,64},{8,72},{16,80},{24,88},{32,96},{40,104},{48,112},{56,120},{... | collective-permute-start | bytes 786440 | tf_op jit(solution)/shard_map/ppermute | solution.py:12
  5.0 3.8 %collective-permute-start.1 = (bf16[2,128,512]{1,2,0:T(8,128)(2,1)S(1)}, bf16[2,128,512]{1,2,0:T(8,128)(2,1)}, u32[]{:S(2)}, u32[]{:S(2)}) collective-permute-start(bf16[2,128,512]{1,2,0:T(8,128)(2,1)S(1)} %copy.54), channel_id=1, source_target_pairs={{0,56},{8,64},{16,72},{24,80},{32,88},{40,96},{48,104},{56,112},{6... | collective-permute-start | bytes 786440 | tf_op jit(solution)/shard_map/ppermute | solution.py:12
  8.7 4.3 %collective-permute-start.7 = (bf16[2,128,512]{1,2,0:T(8,128)(2,1)S(1)}, bf16[2,128,512]{1,2,0:T(8,128)(2,1)}, u32[]{:S(2)}, u32[]{:S(2)}) collective-permute-start(bf16[2,128,512]{1,2,0:T(8,128)(2,1)S(1)} %copy.54), channel_id=1, source_target_pairs={{0,8},{8,16},{16,24},{24,32},{32,40},{40,48},{48,56},{56,64},{64,7... | collective-permute-start | bytes 786440 | tf_op jit(solution)/shard_map/ppermute | solution.py:12
  15.0 2.5 %collective-permute-start.2 = (bf16[2,128,512]{1,2,0:T(8,128)(2,1)S(1)}, bf16[2,128,512]{1,2,0:T(8,128)(2,1)}, u32[]{:S(2)}, u32[]{:S(2)}) collective-permute-start(bf16[2,128,512]{1,2,0:T(8,128)(2,1)S(1)} %copy.54), channel_id=1, source_target_pairs={{0,48},{8,56},{16,64},{24,72},{32,80},{40,88},{48,96},{56,104},{64... | collective-permute-start | bytes 786440 | tf_op jit(solution)/shard_map/ppermute | solution.py:12
  29.6 4.3 %collective-permute-start.5 = (bf16[2,128,512]{1,2,0:T(8,128)(2,1)S(1)}, bf16[2,128,512]{1,2,0:T(8,128)(2,1)S(1)}, u32[]{:S(2)}, u32[]{:S(2)}) collective-permute-start(bf16[2,128,512]{1,2,0:T(8,128)(2,1)S(1)} %copy.54), channel_id=1, source_target_pairs={{0,24},{8,32},{16,40},{24,48},{32,56},{40,64},{48,72},{56,80},{64,... | collective-permute-start | bytes 786440 | tf_op jit(solution)/shard_map/ppermute | solution.py:12
  35.0 14.1 %collective-permute-done.3 = bf16[2,128,512]{1,2,0:T(8,128)(2,1)S(1)} collective-permute-done((bf16[2,128,512]{1,2,0:T(8,128)(2,1)S(1)}, bf16[2,128,512]{1,2,0:T(8,128)(2,1)S(1)}, u32[]{:S(2)}, u32[]{:S(2)}) %collective-permute-start.3) | collective-permute-done | bytes 262176 | tf_op jit(solution)/shard_map/ppermute | solution.py:12
  53.6 2.5 %copy.67 = bf16[1152,4,128]{2,0,1:T(8,128)(2,1)} copy(bf16[1152,4,128]{0,2,1:T(8,128)(2,1)} %bitcast.281) | data formatting | bytes 2359296
  56.1 24.4 %while.30 = (s32[]{:T(128)}, f32[1,128,4,5]{1,3,2,0:T(8,128)S(1)}, f32[1,128,4,5]{1,3,2,0:T(8,128)S(1)}, f32[1,128,4,5,128]{1,4,3,2,0:T(8,128)}, s32[3]{0:T(128)...) while((s32[]{:T(128)}, f32[1,128,4,5]{1,3,2,0:T(8,128)S(1)}, ...), condition=%wide.region_3.4_spmd.clone, body=%wide.region_0.3_spmd.clone.sunk | while | flops 516258944 | bytes 26716976 | solution.py:92
  60.7 2.4 %fusion.113 = f32[1,128,4,5,128]{1,4,3,2,0:T(8,128)S(1)} fusion(f32[4,384,128,5]{2,1,3,0:T(8,128)S(1)} %get-tuple-element.543, f32[128,4,5]{0,2,1:T(8,128)S(1)} %bitcast.278, pred[128,384]{0,1:T(8,128)(4,1)S(1)} %compare_and_fusion.4, f32[1,128,4,5,128]{1,4,3,2,0:T(8,128)S(1)} %copy-done.1, f32[128,4,5]{0,2,1:T(8,128)S(1)} %get-tuple-element.544, ...), kind=kOutput, calls=%fused_computation.14.clone.1 | convolution fusion | flops 256573440 | bytes 7016453 | tf_op jit(solution)/shard_map/while/body/eval_jaxpr/ltgnk,kgd->ltgnd/dot_general | solution.py:80
  68.9 2.4 %fusion.113 = f32[1,128,4,5,128]{1,4,3,2,0:T(8,128)S(1)} fusion(f32[4,384,128,5]{2,1,3,0:T(8,128)S(1)} %get-tuple-element.543, f32[128,4,5]{0,2,1:T(8,128)S(1)} %bitcast.278, pred[128,384]{0,1:T(8,128)(4,1)S(1)} %compare_and_fusion.4, f32[1,128,4,5,128]{1,4,3,2,0:T(8,128)S(1)} %copy-done.1, f32[128,4,5]{0,2,1:T(8,128)S(1)} %get-tuple-element.544, ...), kind=kOutput, calls=%fused_computation.14.clone.1 | convolution fusion | flops 256573440 | bytes 7016453 | tf_op jit(solution)/shard_map/while/body/eval_jaxpr/ltgnk,kgd->ltgnd/dot_general | solution.py:80
  77.0 2.4 %fusion.113 = f32[1,128,4,5,128]{1,4,3,2,0:T(8,128)S(1)} fusion(f32[4,384,128,5]{2,1,3,0:T(8,128)S(1)} %get-tuple-element.543, f32[128,4,5]{0,2,1:T(8,128)S(1)} %bitcast.278, pred[128,384]{0,1:T(8,128)(4,1)S(1)} %compare_and_fusion.4, f32[1,128,4,5,128]{1,4,3,2,0:T(8,128)S(1)} %copy-done.1, f32[128,4,5]{0,2,1:T(8,128)S(1)} %get-tuple-element.544, ...), kind=kOutput, calls=%fused_computation.14.clone.1 | convolution fusion | flops 256573440 | bytes 7016453 | tf_op jit(solution)/shard_map/while/body/eval_jaxpr/ltgnk,kgd->ltgnd/dot_general | solution.py:80
  82.0 33.9 %while.31 = (s32[]{:T(128)}, f32[1,128,4,5,128]{1,4,3,2,0:T(8,128)S(1)}, f32[3,384,4,128]{3,2,1,0:T(4,128)}, f32[3,384,4,128]{3,2,1,0:T(4,128)}, s32[3]{0:T(128)...) while((s32[]{:T(128)}, ...), condition=%wide.region_6.7_spmd.clone, body=%wide.region_5.6_spmd.clone.sunk | while | flops 1268465792 | bytes 23067412 | solution.py:115
  83.6 2.2 %fusion.124 = bf16[1,128,4,5,384]{1,4,3,2,0:T(8,128)(2,1)S(1)} fusion(f32[128,4,5]{0,2,1:T(8,128)S(1)} %bitcast.288, pred[128,384]{0,1:T(8,128)(4,1)S(1)} %compare_and_fusion.5, bf16[1,128,4,5,128]{4,1,3,2,0:T(8,128)(2,1)S(1)} %get-tuple-element.657, bf16[1152,4,128]{2,0,1:T(8,128)(2,1)} %get-tuple-element.653, s32[]{:T(128)S(6)} %select_n.92), kind=kOutput, calls=%fused_computation.41.clone.1 | convolution fusion | flops 256573440 | bytes 3074052 | tf_op jit(solution)/shard_map/while/body/eval_jaxpr/ltgnd,kgd->ltgnk/dot_general | solution.py:67
  91.2 2.2 %copy_dynamic-update-slice_fusion.3 = (f32[3,384,4,128]{3,2,1,0:T(4,128)}, f32[3,384,4,128]{3,2,1,0:T(4,128)}) fusion(f32[3,384,4,128]{3,2,1,0:T(4,128)} %get-tuple-element.632, s32[]{:T(128)S(6)} %copy.140, f32[1,384,4,128]{3,1,2,0:T(8,128)S(1)} %fusion.127, f32[3,384,4,128]{3,2,1,0:T(4,128)} %get-tuple-element.631, f32[1,384,4,128]{3,1,2,0:T(8,128)S(1)} %fusion.128), kind=kLoop, calls=%fused_computation.55.clone.1 | loop fusion | bytes 3145732 | tf_op jit(solution)/shard_map/while/body/jit(dynamic_update_index_in_dim)/dynamic_update_slice | solution.py:115
  94.9 2.2 %fusion.124 = bf16[1,128,4,5,384]{1,4,3,2,0:T(8,128)(2,1)S(1)} fusion(f32[128,4,5]{0,2,1:T(8,128)S(1)} %bitcast.288, pred[128,384]{0,1:T(8,128)(4,1)S(1)} %compare_and_fusion.5, bf16[1,128,4,5,128]{4,1,3,2,0:T(8,128)(2,1)S(1)} %get-tuple-element.657, bf16[1152,4,128]{2,0,1:T(8,128)(2,1)} %get-tuple-element.653, s32[]{:T(128)S(6)} %select_n.92), kind=kOutput, calls=%fused_computation.41.clone.1 | convolution fusion | flops 256573440 | bytes 3074052 | tf_op jit(solution)/shard_map/while/body/eval_jaxpr/ltgnd,kgd->ltgnk/dot_general | solution.py:67
  102.4 2.2 %copy_dynamic-update-slice_fusion.3 = (f32[3,384,4,128]{3,2,1,0:T(4,128)}, f32[3,384,4,128]{3,2,1,0:T(4,128)}) fusion(f32[3,384,4,128]{3,2,1,0:T(4,128)} %get-tuple-element.632, s32[]{:T(128)S(6)} %copy.140, f32[1,384,4,128]{3,1,2,0:T(8,128)S(1)} %fusion.127, f32[3,384,4,128]{3,2,1,0:T(4,128)} %get-tuple-element.631, f32[1,384,4,128]{3,1,2,0:T(8,128)S(1)} %fusion.128), kind=kLoop, calls=%fused_computation.55.clone.1 | loop fusion | bytes 3145732 | tf_op jit(solution)/shard_map/while/body/jit(dynamic_update_index_in_dim)/dynamic_update_slice | solution.py:115
  106.2 2.2 %fusion.124 = bf16[1,128,4,5,384]{1,4,3,2,0:T(8,128)(2,1)S(1)} fusion(f32[128,4,5]{0,2,1:T(8,128)S(1)} %bitcast.288, pred[128,384]{0,1:T(8,128)(4,1)S(1)} %compare_and_fusion.5, bf16[1,128,4,5,128]{4,1,3,2,0:T(8,128)(2,1)S(1)} %get-tuple-element.657, bf16[1152,4,128]{2,0,1:T(8,128)(2,1)} %get-tuple-element.653, s32[]{:T(128)S(6)} %select_n.92), kind=kOutput, calls=%fused_computation.41.clone.1 | convolution fusion | flops 256573440 | bytes 3074052 | tf_op jit(solution)/shard_map/while/body/eval_jaxpr/ltgnd,kgd->ltgnk/dot_general | solution.py:67
  111.8 2.0 fusion.126
  113.8 2.2 %copy_dynamic-update-slice_fusion.3 = (f32[3,384,4,128]{3,2,1,0:T(4,128)}, f32[3,384,4,128]{3,2,1,0:T(4,128)}) fusion(f32[3,384,4,128]{3,2,1,0:T(4,128)} %get-tuple-element.632, s32[]{:T(128)S(6)} %copy.140, f32[1,384,4,128]{3,1,2,0:T(8,128)S(1)} %fusion.127, f32[3,384,4,128]{3,2,1,0:T(4,128)} %get-tuple-element.631, f32[1,384,4,128]{3,1,2,0:T(8,128)S(1)} %fusion.128), kind=kLoop, calls=%fused_computation.55.clone.1 | loop fusion | bytes 3145732 | tf_op jit(solution)/shard_map/while/body/jit(dynamic_update_index_in_dim)/dynamic_update_slice | solution.py:115
  115.9 3.6 %stack.8 = f32[1,9,128,512]{3,2,1,0:T(8,128)} reshape(f32[3,384,4,128]{3,2,1,0:T(4,128)} %get-tuple-element.150) | data formatting | bytes 4718592 | tf_op jit(solution)/shard_map/stack | solution.py:121
  119.6 3.6 %stack.7 = f32[1,9,128,512]{3,2,1,0:T(8,128)} reshape(f32[3,384,4,128]{3,2,1,0:T(4,128)} %get-tuple-element.149) | data formatting | bytes 4718592 | tf_op jit(solution)/shard_map/stack | solution.py:121
  123.2 2.0 constant_dynamic-update-slice_fusion.10
  126.3 7.8 %collective-permute-start.8 = (bf16[2,128,512]{2,1,0:T(8,128)(2,1)S(1)}, bf16[2,128,512]{2,1,0:T(8,128)(2,1)S(1)}, u32[]{:S(2)}, u32[]{:S(2)}) collective-permute-start(bf16[2,128,512]{2,1,0:T(8,128)(2,1)S(1)} %get-tuple-element.374), channel_id=1, source_target_pairs={{8,0},{16,8},{24,16},{32,24},{40,32},{48,40},{56,48},{64,56},{72,6... | collective-permute-start | bytes 786440 | tf_op jit(solution)/shard_map/ppermute | solution.py:12
  134.1 6.5 %collective-permute-start.13 = (bf16[2,128,512]{2,1,0:T(8,128)(2,1)S(1)}, bf16[2,128,512]{2,1,0:T(8,128)(2,1)S(1)}, u32[]{:S(2)}, u32[]{:S(2)}) collective-permute-start(bf16[2,128,512]{2,1,0:T(8,128)(2,1)S(1)} %get-tuple-element.375), channel_id=1, source_target_pairs={{48,0},{56,8},{64,16},{72,24},{80,32},{88,40},{96,48},{104,56},{11... | collective-permute-start | bytes 786440 | tf_op jit(solution)/shard_map/ppermute | solution.py:12
  142.6 2.8 %collective-permute-start.11 = (bf16[2,128,512]{2,1,0:T(8,128)(2,1)S(1)}, bf16[2,128,512]{2,1,0:T(8,128)(2,1)S(1)}, u32[]{:S(2)}, u32[]{:S(2)}) collective-permute-start(bf16[2,128,512]{2,1,0:T(8,128)(2,1)S(1)} %get-tuple-element.377), channel_id=1, source_target_pairs={{32,0},{40,8},{48,16},{56,24},{64,32},{72,40},{80,48},{88,56},{96,... | collective-permute-start | bytes 786440 | tf_op jit(solution)/shard_map/ppermute | solution.py:12
  147.4 2.5 %collective-permute-start.9 = (bf16[2,128,512]{2,1,0:T(8,128)(2,1)S(1)}, bf16[2,128,512]{2,1,0:T(8,128)(2,1)S(1)}, u32[]{:S(2)}, u32[]{:S(2)}) collective-permute-start(bf16[2,128,512]{2,1,0:T(8,128)(2,1)S(1)} %get-tuple-element.379), channel_id=1, source_target_pairs={{16,0},{24,8},{32,16},{40,24},{48,32},{56,40},{64,48},{72,56},{80,... | collective-permute-start | bytes 786440 | tf_op jit(solution)/shard_map/ppermute | solution.py:12
  152.0 20.6 %collective-permute-start.14 = (bf16[2,128,512]{2,1,0:T(8,128)(2,1)S(1)}, bf16[2,128,512]{2,1,0:T(8,128)(2,1)S(1)}, u32[]{:S(2)}, u32[]{:S(2)}) collective-permute-start(bf16[2,128,512]{2,1,0:T(8,128)(2,1)S(1)} %get-tuple-element.381), channel_id=1, source_target_pairs={{56,0},{64,8},{72,16},{80,24},{88,32},{96,40},{104,48},{112,56},{1... | collective-permute-start | bytes 786440 | tf_op jit(solution)/shard_map/ppermute | solution.py:12
  172.5 7.5 %collective-permute-done.11 = bf16[2,128,512]{2,1,0:T(8,128)(2,1)S(1)} collective-permute-done((bf16[2,128,512]{2,1,0:T(8,128)(2,1)S(1)}, bf16[2,128,512]{2,1,0:T(8,128)(2,1)S(1)}, u32[]{:S(2)}, u32[]{:S(2)}) %collective-permute-start.11) | collective-permute-done | bytes 262176 | tf_op jit(solution)/shard_map/ppermute | solution.py:12
  180.1 4.1 %collective-permute-done.10 = bf16[2,128,512]{2,1,0:T(8,128)(2,1)S(1)} collective-permute-done((bf16[2,128,512]{2,1,0:T(8,128)(2,1)S(1)}, bf16[2,128,512]{2,1,0:T(8,128)(2,1)S(1)}, u32[]{:S(2)}, u32[]{:S(2)}) %collective-permute-start.10) | collective-permute-done | bytes 262176 | tf_op jit(solution)/shard_map/ppermute | solution.py:12
  184.2 3.5 %collective-permute-done.14 = bf16[2,128,512]{2,1,0:T(8,128)(2,1)S(1)} collective-permute-done((bf16[2,128,512]{2,1,0:T(8,128)(2,1)S(1)}, bf16[2,128,512]{2,1,0:T(8,128)(2,1)S(1)}, u32[]{:S(2)}, u32[]{:S(2)}) %collective-permute-start.14) | collective-permute-done | bytes 262176 | tf_op jit(solution)/shard_map/ppermute | solution.py:12
  188.7 8.0 %all-to-all-start = ((bf16[8,2,16,512]{3,2,1,0:T(8,128)(2,1)}), bf16[8,2,16,512]{3,2,1,0:T(8,128)(2,1)S(1)}, u32[]{:S(2)}, u32[]{:S(2)}) async-start(bf16[8,2,16,512]{3,2,1,0:T(8,128)(2,1)} %bitcast.213), calls=%async_computation | async-start | bytes 524288 | tf_op jit(solution)/shard_map/all_to_all | solution.py:22
  197.9 9.5 %all-to-all-done = bf16[8,2,16,512]{3,2,1,0:T(8,128)(2,1)S(1)} async-done(((bf16[8,2,16,512]{3,2,1,0:T(8,128)(2,1)}), bf16[8,2,16,512]{3,2,1,0:T(8,128)(2,1)S(1)}, u32[]{:S(2)}, u32[]{:S(2)}) %all-to-all-start) | async-done | bytes 262176 | tf_op jit(solution)/shard_map/all_to_all | solution.py:22
  (131 shorter events, 63.6 us)
Async XLA Ops:
  1.8 22.0 %collective-permute-start = (bf16[2,128,512]{1,2,0:T(8,128)(2,1)S(1)}, bf16[2,128,512]{1,2,0:T(8,128)(2,1)}, u32[]{:S(2)}, u32[]{:S(2)}) collective-permute-start(bf16[2,128,512]{1,2,0:T(8,128)(2,1)S(1)} %copy.54), channel_id=1, source_target_pairs={{0,64},{8,72},{16,80},{24,88},{32,96},{40,104},{48,112},{56,120},{... | collective-permute-start | bytes 786440 | tf_op jit(solution)/shard_map/ppermute | solution.py:12
  5.0 21.7 %collective-permute-start.1 = (bf16[2,128,512]{1,2,0:T(8,128)(2,1)S(1)}, bf16[2,128,512]{1,2,0:T(8,128)(2,1)}, u32[]{:S(2)}, u32[]{:S(2)}) collective-permute-start(bf16[2,128,512]{1,2,0:T(8,128)(2,1)S(1)} %copy.54), channel_id=1, source_target_pairs={{0,56},{8,64},{16,72},{24,80},{32,88},{40,96},{48,104},{56,112},{6... | collective-permute-start | bytes 786440 | tf_op jit(solution)/shard_map/ppermute | solution.py:12
  8.7 42.1 %collective-permute-start.7 = (bf16[2,128,512]{1,2,0:T(8,128)(2,1)S(1)}, bf16[2,128,512]{1,2,0:T(8,128)(2,1)}, u32[]{:S(2)}, u32[]{:S(2)}) collective-permute-start(bf16[2,128,512]{1,2,0:T(8,128)(2,1)S(1)} %copy.54), channel_id=1, source_target_pairs={{0,8},{8,16},{16,24},{24,32},{32,40},{40,48},{48,56},{56,64},{64,7... | collective-permute-start | bytes 786440 | tf_op jit(solution)/shard_map/ppermute | solution.py:12
  13.1 36.7 %collective-permute-start.6 = (bf16[2,128,512]{1,2,0:T(8,128)(2,1)S(1)}, bf16[2,128,512]{1,2,0:T(8,128)(2,1)}, u32[]{:S(2)}, u32[]{:S(2)}) collective-permute-start(bf16[2,128,512]{1,2,0:T(8,128)(2,1)S(1)} %copy.54), channel_id=1, source_target_pairs={{0,16},{8,24},{16,32},{24,40},{32,48},{40,56},{48,64},{56,72},{64,... | collective-permute-start | bytes 786440 | tf_op jit(solution)/shard_map/ppermute | solution.py:12
  15.0 14.6 %collective-permute-start.2 = (bf16[2,128,512]{1,2,0:T(8,128)(2,1)S(1)}, bf16[2,128,512]{1,2,0:T(8,128)(2,1)}, u32[]{:S(2)}, u32[]{:S(2)}) collective-permute-start(bf16[2,128,512]{1,2,0:T(8,128)(2,1)S(1)} %copy.54), channel_id=1, source_target_pairs={{0,48},{8,56},{16,64},{24,72},{32,80},{40,88},{48,96},{56,104},{64... | collective-permute-start | bytes 786440 | tf_op jit(solution)/shard_map/ppermute | solution.py:12
  23.7 25.3 %collective-permute-start.3 = (bf16[2,128,512]{1,2,0:T(8,128)(2,1)S(1)}, bf16[2,128,512]{1,2,0:T(8,128)(2,1)S(1)}, u32[]{:S(2)}, u32[]{:S(2)}) collective-permute-start(bf16[2,128,512]{1,2,0:T(8,128)(2,1)S(1)} %copy.54), channel_id=1, source_target_pairs={{0,40},{8,48},{16,56},{24,64},{32,72},{40,80},{48,88},{56,96},{64,... | collective-permute-start | bytes 786440 | tf_op jit(solution)/shard_map/ppermute | solution.py:12
  26.7 23.0 %collective-permute-start.4 = (bf16[2,128,512]{1,2,0:T(8,128)(2,1)S(1)}, bf16[2,128,512]{1,2,0:T(8,128)(2,1)S(1)}, u32[]{:S(2)}, u32[]{:S(2)}) collective-permute-start(bf16[2,128,512]{1,2,0:T(8,128)(2,1)S(1)} %copy.54), channel_id=1, source_target_pairs={{0,32},{8,40},{16,48},{24,56},{32,64},{40,72},{48,80},{56,88},{64,... | collective-permute-start | bytes 786440 | tf_op jit(solution)/shard_map/ppermute | solution.py:12
  29.6 20.1 %collective-permute-start.5 = (bf16[2,128,512]{1,2,0:T(8,128)(2,1)S(1)}, bf16[2,128,512]{1,2,0:T(8,128)(2,1)S(1)}, u32[]{:S(2)}, u32[]{:S(2)}) collective-permute-start(bf16[2,128,512]{1,2,0:T(8,128)(2,1)S(1)} %copy.54), channel_id=1, source_target_pairs={{0,24},{8,32},{16,40},{24,48},{32,56},{40,64},{48,72},{56,80},{64,... | collective-permute-start | bytes 786440 | tf_op jit(solution)/shard_map/ppermute | solution.py:12
  53.6 2.5 %copy-start.3 = (f32[1,128,4,5]{1,3,2,0:T(8,128)S(1)}, f32[1,128,4,5]{1,3,2,0:T(8,128)}, u32[]{:S(2)}) copy-start(f32[1,128,4,5]{1,3,2,0:T(8,128)} %custom-call.1) | copy-start | bytes 30724
  53.6 2.5 %copy-start.4 = (s32[1152]{0:T(1024)S(1)}, s32[1152]{0:T(1024)}, u32[]{:S(2)}) copy-start(s32[1152]{0:T(1024)} %get-tuple-element.617) | copy-start | bytes 13828
  53.6 2.5 %copy-start.5 = (s32[1152]{0:T(1024)S(1)}, s32[1152]{0:T(1024)}, u32[]{:S(2)}) copy-start(s32[1152]{0:T(1024)} %get-tuple-element.616) | copy-start | bytes 13828
  53.6 2.5 %copy-start.6 = (s32[128]{0:T(128)S(1)}, s32[128]{0:T(128)}, u32[]{:S(2)}) copy-start(s32[128]{0:T(128)} %dynamic_slice.38) | copy-start | bytes 1540
  59.4 1.3 copy-start.1
  63.2 1.1 copy-start.2
  67.5 1.3 copy-start.1
  71.3 1.1 copy-start.2
  75.7 1.3 copy-start.1
  79.4 1.1 copy-start.2
  123.2 2.4 %copy-start = (f32[1,9,128,512]{3,2,1,0:T(8,128)S(1)}, f32[1,9,128,512]{3,2,1,0:T(8,128)}, u32[]{:S(2)}) copy-start(f32[1,9,128,512]{3,2,1,0:T(8,128)} %stack.8) | copy-start | bytes 7077892
  126.3 21.1 %collective-permute-start.8 = (bf16[2,128,512]{2,1,0:T(8,128)(2,1)S(1)}, bf16[2,128,512]{2,1,0:T(8,128)(2,1)S(1)}, u32[]{:S(2)}, u32[]{:S(2)}) collective-permute-start(bf16[2,128,512]{2,1,0:T(8,128)(2,1)S(1)} %get-tuple-element.374), channel_id=1, source_target_pairs={{8,0},{16,8},{24,16},{32,24},{40,32},{48,40},{56,48},{64,56},{72,6... | collective-permute-start | bytes 786440 | tf_op jit(solution)/shard_map/ppermute | solution.py:12
  134.1 15.7 %collective-permute-start.13 = (bf16[2,128,512]{2,1,0:T(8,128)(2,1)S(1)}, bf16[2,128,512]{2,1,0:T(8,128)(2,1)S(1)}, u32[]{:S(2)}, u32[]{:S(2)}) collective-permute-start(bf16[2,128,512]{2,1,0:T(8,128)(2,1)S(1)} %get-tuple-element.375), channel_id=1, source_target_pairs={{48,0},{56,8},{64,16},{72,24},{80,32},{88,40},{96,48},{104,56},{11... | collective-permute-start | bytes 786440 | tf_op jit(solution)/shard_map/ppermute | solution.py:12
  140.7 11.3 %collective-permute-start.12 = (bf16[2,128,512]{2,1,0:T(8,128)(2,1)S(1)}, bf16[2,128,512]{2,1,0:T(8,128)(2,1)S(1)}, u32[]{:S(2)}, u32[]{:S(2)}) collective-permute-start(bf16[2,128,512]{2,1,0:T(8,128)(2,1)S(1)} %get-tuple-element.376), channel_id=1, source_target_pairs={{40,0},{48,8},{56,16},{64,24},{72,32},{80,40},{88,48},{96,56},{104... | collective-permute-start | bytes 786440 | tf_op jit(solution)/shard_map/ppermute | solution.py:12
  142.6 37.5 %collective-permute-start.11 = (bf16[2,128,512]{2,1,0:T(8,128)(2,1)S(1)}, bf16[2,128,512]{2,1,0:T(8,128)(2,1)S(1)}, u32[]{:S(2)}, u32[]{:S(2)}) collective-permute-start(bf16[2,128,512]{2,1,0:T(8,128)(2,1)S(1)} %get-tuple-element.377), channel_id=1, source_target_pairs={{32,0},{40,8},{48,16},{56,24},{64,32},{72,40},{80,48},{88,56},{96,... | collective-permute-start | bytes 786440 | tf_op jit(solution)/shard_map/ppermute | solution.py:12
  145.4 38.7 %collective-permute-start.10 = (bf16[2,128,512]{2,1,0:T(8,128)(2,1)S(1)}, bf16[2,128,512]{2,1,0:T(8,128)(2,1)S(1)}, u32[]{:S(2)}, u32[]{:S(2)}) collective-permute-start(bf16[2,128,512]{2,1,0:T(8,128)(2,1)S(1)} %get-tuple-element.378), channel_id=1, source_target_pairs={{24,0},{32,8},{40,16},{48,24},{56,32},{64,40},{72,48},{80,56},{88,... | collective-permute-start | bytes 786440 | tf_op jit(solution)/shard_map/ppermute | solution.py:12
  147.4 36.8 %collective-permute-start.9 = (bf16[2,128,512]{2,1,0:T(8,128)(2,1)S(1)}, bf16[2,128,512]{2,1,0:T(8,128)(2,1)S(1)}, u32[]{:S(2)}, u32[]{:S(2)}) collective-permute-start(bf16[2,128,512]{2,1,0:T(8,128)(2,1)S(1)} %get-tuple-element.379), channel_id=1, source_target_pairs={{16,0},{24,8},{32,16},{40,24},{48,32},{56,40},{64,48},{72,56},{80,... | collective-permute-start | bytes 786440 | tf_op jit(solution)/shard_map/ppermute | solution.py:12
  149.9 34.3 %collective-permute-start.15 = (bf16[2,128,512]{2,1,0:T(8,128)(2,1)S(1)}, bf16[2,128,512]{2,1,0:T(8,128)(2,1)S(1)}, u32[]{:S(2)}, u32[]{:S(2)}) collective-permute-start(bf16[2,128,512]{2,1,0:T(8,128)(2,1)S(1)} %get-tuple-element.380), channel_id=1, source_target_pairs={{64,0},{72,8},{80,16},{88,24},{96,32},{104,40},{112,48},{120,56},{... | collective-permute-start | bytes 786440 | tf_op jit(solution)/shard_map/ppermute | solution.py:12
  152.0 35.7 %collective-permute-start.14 = (bf16[2,128,512]{2,1,0:T(8,128)(2,1)S(1)}, bf16[2,128,512]{2,1,0:T(8,128)(2,1)S(1)}, u32[]{:S(2)}, u32[]{:S(2)}) collective-permute-start(bf16[2,128,512]{2,1,0:T(8,128)(2,1)S(1)} %get-tuple-element.381), channel_id=1, source_target_pairs={{56,0},{64,8},{72,16},{80,24},{88,32},{96,40},{104,48},{112,56},{1... | collective-permute-start | bytes 786440 | tf_op jit(solution)/shard_map/ppermute | solution.py:12
  188.7 18.6 %all-to-all-start = ((bf16[8,2,16,512]{3,2,1,0:T(8,128)(2,1)}), bf16[8,2,16,512]{3,2,1,0:T(8,128)(2,1)S(1)}, u32[]{:S(2)}, u32[]{:S(2)}) async-start(bf16[8,2,16,512]{3,2,1,0:T(8,128)(2,1)} %bitcast.213), calls=%async_computation | async-start | bytes 524288 | tf_op jit(solution)/shard_map/all_to_all | solution.py:22
where the time goes:
time: 210 us; the launch traced here: 208 us
  starting transfers between devices  77.7 us (37%)
  local copies, waits for them, and re-layouts  42.3 us (20%)
  waiting for transfers between devices  39.5 us (19%)
  matrix products  34.8 us (17%)
  other arithmetic  8.3 us (4%)
  loops' own time  4.33 us (2%)
    ppermute x16, starting transfers between devices, from_behind(): lax.ppermute(value, axis, [(source, source + steps) for source in range(f...  69.8 us
    ppermute x16, waiting for transfers between devices, from_behind(): lax.ppermute(value, axis, [(source, source + steps) for source in range(f...  30 us
    unnamed x26, local copies, waits for them, and re-layouts  15.8 us
    dot_general x6, matrix products, block_scores(): jnp.einsum('ltgnd,kgd->ltgnk', qrows, kpart, preferred_element_type=jnp.f...  11.9 us
    all_to_all x1, waiting for transfers between devices, summed_on_arrival(): lax.all_to_all(blocks, axis, split_axis=0, concat_axis=0, tiled=True)  9.5 us
    all_to_all x1, starting transfers between devices, summed_on_arrival(): lax.all_to_all(blocks, axis, split_axis=0, concat_axis=0, tiled=True)  7.95 us
    another operation x3, local copies, waits for them, and re-layouts, body(): jnp.stack([dkeys.reshape(total, kv_width), dvalues.reshape(total, kv_widt...  7.46 us
    dot_general x3, matrix products, forward_step(): jnp.einsum('ltgnk,kgd->ltgnd', weights, vpart.astype(jnp.float32))  7.22 us
  transfers between devices with their start and end apart: 17, of which 7 were waited for; matrix products, arithmetic and copies ran while one was open for 6% of the time, Pallas kernels for 0%

commit v1 on v0

v1 whole, which is shorter than its diff:
```python
import functools, math
import jax, jax.numpy as jnp
from jax import lax
from jax.sharding import PartitionSpec as P
from jax.experimental import pallas as pl
from jax.experimental.pallas import tpu as pltpu
HD=128
TOK=128
def attn_kernel(heads_in, groups, nb, CH, qd_ref, s_in_ref, r_in_ref, bias_ref, dq_ref, ds_out_ref, dr_out_ref,
                k_ref, v_ref, kt_ref, sc_ref, dp_ref, dsb_ref, dk_ref, dv_ref):
    nkeys = nb*TOK
    scale = HD ** -0.5
    c2 = scale*math.log2(math.e)
    for b in range(nb):
        src = s_in_ref if b%2==0 else r_in_ref
        k_ref[b*TOK:(b+1)*TOK,:] = src[b//2,0]
        v_ref[b*TOK:(b+1)*TOK,:] = src[b//2,1]
        kt_ref[:, b*TOK:(b+1)*TOK] = src[b//2,0].T
    dk_ref[...] = jnp.zeros_like(dk_ref)
    dv_ref[...] = jnp.zeros_like(dv_ref)
    def step(p, carry):
        places=[]
        for o in (0,1):
            h = 2*p+o
            l = h//groups
            places.append((l, pl.ds(pl.multiple_of((h-l*groups)*HD,HD),HD)))
        (la,na),(lb,nb_)=places
        qq = jnp.concatenate([qd_ref[la,0,:,na], qd_ref[lb,0,:,nb_]],axis=0)
        dd = jnp.concatenate([qd_ref[la,1,:,na], qd_ref[lb,1,:,nb_]],axis=0)
        nt = (((1,),(1,)),((),()))
        top = jnp.full((8,2*TOK),-3e38,jnp.float32)
        for c in range(0,nkeys,CH):
            s = lax.dot_general(k_ref[c:c+CH,:], qq, nt, preferred_element_type=jnp.float32)
            bias = bias_ref[c:c+CH,:]
            s = s*c2 + jnp.concatenate([bias,bias],axis=1)
            sc_ref[c:c+CH,:] = s
            top = jnp.maximum(top, jnp.max(s.reshape(CH//8,8,2*TOK),axis=0))
        top = jnp.max(top,axis=0,keepdims=True)
        tot = jnp.zeros((8,2*TOK),jnp.float32)
        dl = jnp.zeros((8,2*TOK),jnp.float32)
        for c in range(0,nkeys,CH):
            dp = lax.dot_general(v_ref[c:c+CH,:], dd, nt, preferred_element_type=jnp.float32)
            e = jnp.exp2(sc_ref[c:c+CH,:]-top)
            tot = tot + jnp.sum(e.reshape(CH//8,8,2*TOK),axis=0)
            dl = dl + jnp.sum((e*dp).reshape(CH//8,8,2*TOK),axis=0)
            sc_ref[c:c+CH,:] = e
            dp_ref[c:c+CH,:] = dp
        rec = 1.0/jnp.sum(tot,axis=0,keepdims=True)
        delta = jnp.sum(dl,axis=0,keepdims=True)*rec
        for c in range(0,nkeys,CH):
            prob = (sc_ref[c:c+CH,:]*rec).astype(jnp.bfloat16)
            ds = (prob.astype(jnp.float32)*(dp_ref[c:c+CH,:]-delta)).astype(jnp.bfloat16)
            dsb_ref[c:c+CH,:] = ds
            dv_ref[c:c+CH,:] += jnp.dot(prob, dd, preferred_element_type=jnp.float32)
            dk_ref[c:c+CH,:] += jnp.dot(ds, qq, preferred_element_type=jnp.float32)
        dqt = jnp.dot(kt_ref[...], dsb_ref[...], preferred_element_type=jnp.float32)
        dqq = (dqt.T*scale).astype(jnp.bfloat16)
        dq_ref[la,:,na] = dqq[:TOK]
        dq_ref[lb,:,nb_] = dqq[TOK:]
        return carry
    lax.fori_loop(0, heads_in//2, step, 0)
    for b in range(nb):
        dst = ds_out_ref if b%2==0 else dr_out_ref
        dst[b//2,0] = (dk_ref[b*TOK:(b+1)*TOK,:]*scale).astype(dst.dtype)
        dst[b//2,1] = dv_ref[b*TOK:(b+1)*TOK,:].astype(dst.dtype)

def attn(qd, s_in, r_in, bias, CH=384):
    L=qd.shape[0]; groups=qd.shape[3]//HD
    ns, nr = s_in.shape[0], r_in.shape[0]
    nb=ns+nr; nk=nb*TOK
    body=functools.partial(attn_kernel, L*groups, groups, nb, CH)
    flops=5*2*L*TOK*groups*HD*nk
    vm=pl.BlockSpec(memory_space=pltpu.VMEM)
    return pl.pallas_call(body,
        out_shape=(jax.ShapeDtypeStruct((L,TOK,groups*HD),jnp.bfloat16),
                   jax.ShapeDtypeStruct((ns,2,TOK,HD),jnp.float32),
                   jax.ShapeDtypeStruct((nr,2,TOK,HD),jnp.bfloat16)),
        in_specs=[vm]*4, out_specs=(vm,)*3,
        scratch_shapes=[pltpu.VMEM((nk,HD),jnp.bfloat16),pltpu.VMEM((nk,HD),jnp.bfloat16),pltpu.VMEM((HD,nk),jnp.bfloat16),
            pltpu.VMEM((nk,2*TOK),jnp.float32),pltpu.VMEM((nk,2*TOK),jnp.float32),pltpu.VMEM((nk,2*TOK),jnp.bfloat16),
            pltpu.VMEM((nk,HD),jnp.float32),pltpu.VMEM((nk,HD),jnp.float32)],
        cost_estimate=pl.CostEstimate(flops=flops,bytes_accessed=4*1024*1024,transcendentals=L*TOK*groups*nk),
        compiler_params=pltpu.CompilerParams(vmem_limit_bytes=32*1024*1024),
        name="attn_bwd")(qd,s_in,r_in,bias)


def chip_back(value, chips):
    count = lax.axis_size("ctx")
    steps = 2 * chips
    first, last = (max(0, -steps), min(count, count - steps))
    return lax.ppermute(value, "ctx", [(s, s + steps) for s in range(first, last)])


def other_core(value):
    return lax.ppermute(value, "ctx", [(s, s ^ 1) for s in range(lax.axis_size("ctx"))])


def body(queries, grad_out, keys_values, doc_ids):
    layers, tok_rows, width = queries.shape
    kv_width = keys_values.shape[2]
    heads_kv = kv_width // HD
    part = width // heads_kv
    count = lax.axis_size("ctx")
    sections = lax.axis_size("section")
    chips = count // 8
    place = lax.axis_index("ctx")
    core = place % 2
    head = lax.axis_index("section") % heads_kv
    xgroups = [[g + i for i in range(heads_kv)] for g in range(0, sections, heads_kv)]

    qd = jnp.stack([queries[0], grad_out[0]]).reshape(2, tok_rows, heads_kv, part)
    qd = qd.transpose(2, 0, 1, 3)
    qd = lax.all_to_all(qd, "section", 0, 0, axis_index_groups=xgroups, tiled=True)

    own = lax.dynamic_slice_in_dim(keys_values, head * HD, HD, 2)
    same = jnp.stack([chip_back(own, d) for d in range(chips, 0, -1)] + [own])
    cross = other_core(lax.dynamic_slice_in_dim(same, 1 - core, chips, 0))

    span = 2 * chips + 1
    total = span * tok_rows
    first = place * tok_rows
    qdoc = lax.dynamic_slice_in_dim(doc_ids, first, tok_rows, 0)
    padded = jnp.concatenate([jnp.full((total - tok_rows,), -1, jnp.int32), doc_ids])
    kdoc = lax.dynamic_slice_in_dim(padded, first, total, 0)
    kat = jnp.arange(total, dtype=jnp.int32) - (total - tok_rows)
    qat = jnp.arange(tok_rows, dtype=jnp.int32)
    seen = (kat[:, None] <= qat[None, :]) & (kdoc[:, None] == qdoc[None, :])
    bias = jnp.where(seen, 0.0, -1e30).astype(jnp.float32)

    dq, dsame, dcross = attn(qd, same, cross, bias)

    arrived = other_core(dcross).astype(jnp.float32)
    zero = jnp.zeros((1,) + arrived.shape[1:], jnp.float32)
    dsame = dsame + jnp.where(
        core == 1, jnp.concatenate([arrived, zero]), jnp.concatenate([zero, arrived])
    )
    grad = dsame[chips]
    for d in range(chips, 0, -1):
        grad = grad + chip_back(dsame[chips - d].astype(jnp.bfloat16), -d).astype(jnp.float32)

    dq = lax.all_to_all(dq, "section", 0, 0, axis_index_groups=xgroups, tiled=True)
    grad_queries = dq.transpose(1, 0, 2).reshape(1, tok_rows, width)

    rows = tok_rows // sections
    pieces = grad.astype(jnp.bfloat16).reshape(2, sections, rows, HD).transpose(1, 0, 2, 3)
    got = lax.all_to_all(pieces, "section", 0, 0, tiled=True).astype(jnp.float32)
    got = got.reshape(sections // heads_kv, heads_kv, 2, rows, HD).sum(axis=0)
    grad_kv = got.transpose(1, 2, 0, 3).reshape(2, rows, kv_width).astype(jnp.bfloat16)
    return (grad_queries, grad_kv)


def solution(mesh):
    return jax.shard_map(
        body,
        mesh=mesh,
        in_specs=(P("section", "ctx", None), P("section", "ctx", None), P(None, "ctx", None), P()),
        out_specs=(P("section", "ctx", None), P(None, ("ctx", "section"), None)),
        check_vma=False,
    )
```

time: 210 us -> 107 us (0.51)
  the two profiles are of different devices: /device:TPU:105 before, /device:TPU:16 now
where the time goes in v1:
time: 107 us
  starting transfers between devices  34.6 us (32%)
  waiting for transfers between devices  31.1 us (29%)
  blocking collectives  17 us (16%)
  Pallas kernels  15 us (14%)
  local copies, waits for them, and re-layouts  7.18 us (7%)
    ppermute x8, starting transfers between devices, chip_back(): lax.ppermute(value, 'ctx', [(s, s + steps) for s in range(first, last)])  26.6 us
    all_to_all x1, blocking collectives, body(): lax.all_to_all(pieces, 'section', 0, 0, tiled=True).astype(jnp.float32)  17 us
    pallas_call x1, Pallas kernels, attn(): pl.pallas_call(body, out_shape=(jax.ShapeDtypeStruct((L, TOK, groups * HD...  15 us
    all_to_all x1, waiting for transfers between devices, body(): lax.all_to_all(qd, 'section', 0, 0, axis_index_groups=xgroups, tiled=True)  14.3 us
    all_to_all x1, waiting for transfers between devices, body(): lax.all_to_all(dq, 'section', 0, 0, axis_index_groups=xgroups, tiled=True)  8.11 us
    ppermute x8, waiting for transfers between devices, chip_back(): lax.ppermute(value, 'ctx', [(s, s + steps) for s in range(first, last)])  6.02 us
    all_to_all x1, starting transfers between devices, body(): lax.all_to_all(qd, 'section', 0, 0, axis_index_groups=xgroups, tiled=True)  4.42 us
    all_to_all x1, starting transfers between devices, body(): lax.all_to_all(dq, 'section', 0, 0, axis_index_groups=xgroups, tiled=True)  3.48 us
  transfers between devices with their start and end apart: 12, of which 6 were waited for; matrix products, arithmetic and copies ran while one was open for 5% of the time, Pallas kernels for 0%

profile of v1, /device:TPU:16, one launch (start us, length us, event | category | flops | bytes accessed | tf_op | source)
XLA Modules:
  0.0 106.6 jit_solution(11229628682526235249)
XLA Ops:
  0.7 0.9 constant_dynamic-slice_fusion.1
  1.6 3.8 %collective-permute-start.3 = (bf16[2,128,128]{2,1,0:T(8,128)(2,1)S(1)}, bf16[2,128,128]{2,1,0:T(8,128)(2,1)S(1)}, u32[]{:S(2)}, u32[]{:S(2)}) collective-permute-start(bf16[2,128,128]{2,1,0:T(8,128)(2,1)S(1)} %constant_dynamic-slice_fusion.1), channel_id=1, source_target_pairs={{0,16},{8,24},{16,32},{24,40},{32,48},{40,56},{48,64},{56,72},{64,... | collective-permute-start | bytes 196616 | tf_op jit(solution)/shard_map/ppermute | solution.py:91
  5.4 5.2 %collective-permute-start.2 = (bf16[2,128,128]{2,1,0:T(8,128)(2,1)S(1)}, bf16[2,128,128]{2,1,0:T(8,128)(2,1)S(1)}, u32[]{:S(2)}, u32[]{:S(2)}) collective-permute-start(bf16[2,128,128]{2,1,0:T(8,128)(2,1)S(1)} %constant_dynamic-slice_fusion.1), channel_id=1, source_target_pairs={{0,32},{8,40},{16,48},{24,56},{32,64},{40,72},{48,80},{56,88},{64,... | collective-permute-start | bytes 196616 | tf_op jit(solution)/shard_map/ppermute | solution.py:91
  10.6 3.6 %collective-permute-start.1 = (bf16[2,128,128]{2,1,0:T(8,128)(2,1)S(1)}, bf16[2,128,128]{2,1,0:T(8,128)(2,1)S(1)}, u32[]{:S(2)}, u32[]{:S(2)}) collective-permute-start(bf16[2,128,128]{2,1,0:T(8,128)(2,1)S(1)} %constant_dynamic-slice_fusion.1), channel_id=1, source_target_pairs={{0,48},{8,56},{16,64},{24,72},{32,80},{40,88},{48,96},{56,104},{64... | collective-permute-start | bytes 196616 | tf_op jit(solution)/shard_map/ppermute | solution.py:91
  14.2 1.9 %collective-permute-start = (bf16[2,128,128]{2,1,0:T(8,128)(2,1)S(1)}, bf16[2,128,128]{2,1,0:T(8,128)(2,1)S(1)}, u32[]{:S(2)}, u32[]{:S(2)}) collective-permute-start(bf16[2,128,128]{2,1,0:T(8,128)(2,1)S(1)} %constant_dynamic-slice_fusion.1), channel_id=1, source_target_pairs={{0,64},{8,72},{16,80},{24,88},{32,96},{40,104},{48,112},{56,120},{... | collective-permute-start | bytes 196616 | tf_op jit(solution)/shard_map/ppermute | solution.py:91
  16.1 1.4 %copy.18 = bf16[1,128,2560]{1,2,0:T(8,128)(2,1)S(1)} copy(bf16[1,128,2560]{2,1,0:T(8,128)(2,1)} %param.4) | data formatting | bytes 1310720 | tf_op args[0]
  17.6 0.3 copy.19
  17.9 0.1 pad_maximum_fusion
  18.0 1.5 %copy.20 = bf16[2,128,4,640]{3,1,0,2:T(8,128)(2,1)} copy(bf16[2,128,4,640]{1,3,2,0:T(8,128)(2,1)S(1)} %bitcast.46) | data formatting | bytes 2621440 | tf_op jit(solution)/shard_map/reshape | solution.py:111
  19.5 4.4 %all-to-all-start = ((bf16[4,2,128,640]{3,2,1,0:T(8,128)(2,1)}), bf16[4,2,128,640]{3,2,1,0:T(8,128)(2,1)S(1)}, u32[]{:S(2)}, u32[]{:S(2)}) async-start(bf16[4,2,128,640]{3,2,1,0:T(8,128)(2,1)} %bitcast.1), calls=%async_computation | async-start | bytes 2621440 | tf_op jit(solution)/shard_map/all_to_all | solution.py:113
  23.9 0.1 dynamic_slice.15
  24.0 0.1 pad_dynamic-slice_fusion
  24.2 0.9 bitcast_dynamic-update-slice_fusion.s_in_ref
  25.1 0.1 collective-permute-start.4
  25.2 0.4 fusion.1.bias_ref
  25.6 1.1 %collective-permute-done.4.r_in_ref = bf16[4,2,128,128]{3,2,1,0:T(8,128)(2,1)S(1)} collective-permute-done((bf16[4,2,128,128]{3,2,1,0:T(8,128)(2,1)S(1)}, bf16[4,2,128,128]{3,2,1,0:T(8,128)(2,1)S(1)}, u32[]{:S(2)}, u32[]{:S(2)}) %collective-permute-start.4) | collective-permute-done | bytes 262176 | tf_op jit(solution)/shard_map/ppermute | solution.py:95
  26.7 14.3 %all-to-all-done.qd_ref = bf16[4,2,128,640]{3,2,1,0:T(8,128)(2,1)S(1)} async-done(((bf16[4,2,128,640]{3,2,1,0:T(8,128)(2,1)}), bf16[4,2,128,640]{3,2,1,0:T(8,128)(2,1)S(1)}, u32[]{:S(2)}, u32[]{:S(2)}) %all-to-all-start) | async-done | bytes 1310752 | tf_op jit(solution)/shard_map/all_to_all | solution.py:113
  41.0 15.0 %attn_bwd.1 = (bf16[4,128,640]{2,1,0:T(8,128)(2,1)}, f32[5,2,128,128]{3,2,1,0:T(8,128)S(1)}, bf16[4,2,128,128]{3,2,1,0:T(8,128)(2,1)S(1)}) custom-call(bf16[4,2,128,640]{3,2,1,0:T(8,128)(2,1)S(1)} %all-to-all-done.qd_ref, bf16[5,2,128,128]{3,2,1,0:T(8,128)(2,1)S(1)} %bitcast_dynamic-update-slice_fusion.s_in_ref, ...), custom_call_target="tpu_custom_call" | custom-call | flops 3774873600 | bytes 4194304 | tf_op jit(solution)/shard_map/attn_bwd/pallas_call | solution.py:74
  56.0 1.5 %collective-permute-done.5 = bf16[4,2,128,128]{3,2,1,0:T(8,128)(2,1)S(1)} collective-permute-done((bf16[4,2,128,128]{3,2,1,0:T(8,128)(2,1)S(1)}, bf16[4,2,128,128]{3,2,1,0:T(8,128)(2,1)S(1)}, u32[]{:S(2)}, u32[]{:S(2)}) %collective-permute-start.5) | collective-permute-done | bytes 262176 | tf_op jit(solution)/shard_map/ppermute | solution.py:95
  57.6 0.1 fusion.7
  57.7 3.6 %collective-permute-start.6 = (bf16[2,128,128]{2,1,0:T(8,128)(2,1)S(1)}, bf16[2,128,128]{2,1,0:T(8,128)(2,1)S(1)}, u32[]{:S(2)}, u32[]{:S(2)}) collective-permute-start(bf16[2,128,128]{2,1,0:T(8,128)(2,1)S(1)} %get-tuple-element.16), channel_id=1, source_target_pairs={{64,0},{72,8},{80,16},{88,24},{96,32},{104,40},{112,48},{120,56},{... | collective-permute-start | bytes 196616 | tf_op jit(solution)/shard_map/ppermute | solution.py:91
  61.4 2.9 %collective-permute-start.9 = (bf16[2,128,128]{2,1,0:T(8,128)(2,1)S(1)}, bf16[2,128,128]{2,1,0:T(8,128)(2,1)S(1)}, u32[]{:S(2)}, u32[]{:S(2)}) collective-permute-start(bf16[2,128,128]{2,1,0:T(8,128)(2,1)S(1)} %get-tuple-element.17), channel_id=1, source_target_pairs={{16,0},{24,8},{32,16},{40,24},{48,32},{56,40},{64,48},{72,56},{80,... | collective-permute-start | bytes 196616 | tf_op jit(solution)/shard_map/ppermute | solution.py:91
  64.3 3.6 %collective-permute-start.8 = (bf16[2,128,128]{2,1,0:T(8,128)(2,1)S(1)}, bf16[2,128,128]{2,1,0:T(8,128)(2,1)S(1)}, u32[]{:S(2)}, u32[]{:S(2)}) collective-permute-start(bf16[2,128,128]{2,1,0:T(8,128)(2,1)S(1)} %get-tuple-element.18), channel_id=1, source_target_pairs={{32,0},{40,8},{48,16},{56,24},{64,32},{72,40},{80,48},{88,56},{96,... | collective-permute-start | bytes 196616 | tf_op jit(solution)/shard_map/ppermute | solution.py:91
  67.9 1.9 %collective-permute-start.7 = (bf16[2,128,128]{2,1,0:T(8,128)(2,1)S(1)}, bf16[2,128,128]{2,1,0:T(8,128)(2,1)S(1)}, u32[]{:S(2)}, u32[]{:S(2)}) collective-permute-start(bf16[2,128,128]{2,1,0:T(8,128)(2,1)S(1)} %get-tuple-element.19), channel_id=1, source_target_pairs={{48,0},{56,8},{64,16},{72,24},{80,32},{88,40},{96,48},{104,56},{11... | collective-permute-start | bytes 196616 | tf_op jit(solution)/shard_map/ppermute | solution.py:91
  69.8 2.2 %collective-permute-done.8 = bf16[2,128,128]{2,1,0:T(8,128)(2,1)S(1)} collective-permute-done((bf16[2,128,128]{2,1,0:T(8,128)(2,1)S(1)}, bf16[2,128,128]{2,1,0:T(8,128)(2,1)S(1)}, u32[]{:S(2)}, u32[]{:S(2)}) %collective-permute-start.8) | collective-permute-done | bytes 65568 | tf_op jit(solution)/shard_map/ppermute | solution.py:91
  72.1 3.8 %collective-permute-done.7 = bf16[2,128,128]{2,1,0:T(8,128)(2,1)S(1)} collective-permute-done((bf16[2,128,128]{2,1,0:T(8,128)(2,1)S(1)}, bf16[2,128,128]{2,1,0:T(8,128)(2,1)S(1)}, u32[]{:S(2)}, u32[]{:S(2)}) %collective-permute-start.7) | collective-permute-done | bytes 65568 | tf_op jit(solution)/shard_map/ppermute | solution.py:91
  75.9 17.0 %all_to_all.15 = bf16[8,2,16,128]{3,2,1,0:T(8,128)(2,1)S(1)} all-to-all(bf16[8,2,16,128]{3,2,1,0:T(8,128)(2,1)S(1)} %bitcast.51), channel_id=1, replica_groups=mesh['ctx'=32,'section'=8] {'section'}, dimensions={0} | all-to-all | bytes 131072 | tf_op jit(solution)/shard_map/all_to_all | solution.py:146
  92.9 3.5 %all-to-all-start.1 = ((bf16[4,128,640]{2,1,0:T(8,128)(2,1)}), bf16[4,128,640]{2,1,0:T(8,128)(2,1)S(1)}, u32[]{:S(2)}, u32[]{:S(2)}) async-start(bf16[4,128,640]{2,1,0:T(8,128)(2,1)} %get-tuple-element.5), calls=%async_computation.1 | async-start | bytes 1310720 | tf_op jit(solution)/shard_map/all_to_all | solution.py:141
  96.4 0.6 copy_bitcast_fusion.1
  97.1 8.1 %all-to-all-done.1 = bf16[4,128,640]{2,1,0:T(8,128)(2,1)S(1)} async-done(((bf16[4,128,640]{2,1,0:T(8,128)(2,1)}), bf16[4,128,640]{2,1,0:T(8,128)(2,1)S(1)}, u32[]{:S(2)}, u32[]{:S(2)}) %all-to-all-start.1) | async-done | bytes 655392 | tf_op jit(solution)/shard_map/all_to_all | solution.py:141
  105.2 0.3 copy.21
  105.5 1.1 %copy.25 = bf16[1,128,2560]{2,1,0:T(8,128)(2,1)} copy(bf16[1,128,2560]{1,2,0:T(8,128)(2,1)S(1)} %bitcast.48) | data formatting | bytes 1310720
  (21 shorter events, 0.2 us)
Async XLA Ops:
  0.6 16.9 %copy-start = (bf16[1,128,2560]{2,1,0:T(8,128)(2,1)S(1)}, bf16[1,128,2560]{2,1,0:T(8,128)(2,1)}, u32[]{:S(2)}) copy-start(bf16[1,128,2560]{2,1,0:T(8,128)(2,1)} %param.5) | copy-start | bytes 1966084
  1.6 22.6 %collective-permute-start.3 = (bf16[2,128,128]{2,1,0:T(8,128)(2,1)S(1)}, bf16[2,128,128]{2,1,0:T(8,128)(2,1)S(1)}, u32[]{:S(2)}, u32[]{:S(2)}) collective-permute-start(bf16[2,128,128]{2,1,0:T(8,128)(2,1)S(1)} %constant_dynamic-slice_fusion.1), channel_id=1, source_target_pairs={{0,16},{8,24},{16,32},{24,40},{32,48},{40,56},{48,64},{56,72},{64,... | collective-permute-start | bytes 196616 | tf_op jit(solution)/shard_map/ppermute | solution.py:91
  5.4 18.7 %collective-permute-start.2 = (bf16[2,128,128]{2,1,0:T(8,128)(2,1)S(1)}, bf16[2,128,128]{2,1,0:T(8,128)(2,1)S(1)}, u32[]{:S(2)}, u32[]{:S(2)}) collective-permute-start(bf16[2,128,128]{2,1,0:T(8,128)(2,1)S(1)} %constant_dynamic-slice_fusion.1), channel_id=1, source_target_pairs={{0,32},{8,40},{16,48},{24,56},{32,64},{40,72},{48,80},{56,88},{64,... | collective-permute-start | bytes 196616 | tf_op jit(solution)/shard_map/ppermute | solution.py:91
  10.6 13.5 %collective-permute-start.1 = (bf16[2,128,128]{2,1,0:T(8,128)(2,1)S(1)}, bf16[2,128,128]{2,1,0:T(8,128)(2,1)S(1)}, u32[]{:S(2)}, u32[]{:S(2)}) collective-permute-start(bf16[2,128,128]{2,1,0:T(8,128)(2,1)S(1)} %constant_dynamic-slice_fusion.1), channel_id=1, source_target_pairs={{0,48},{8,56},{16,64},{24,72},{32,80},{40,88},{48,96},{56,104},{64... | collective-permute-start | bytes 196616 | tf_op jit(solution)/shard_map/ppermute | solution.py:91
  14.2 9.9 %collective-permute-start = (bf16[2,128,128]{2,1,0:T(8,128)(2,1)S(1)}, bf16[2,128,128]{2,1,0:T(8,128)(2,1)S(1)}, u32[]{:S(2)}, u32[]{:S(2)}) collective-permute-start(bf16[2,128,128]{2,1,0:T(8,128)(2,1)S(1)} %constant_dynamic-slice_fusion.1), channel_id=1, source_target_pairs={{0,64},{8,72},{16,80},{24,88},{32,96},{40,104},{48,112},{56,120},{... | collective-permute-start | bytes 196616 | tf_op jit(solution)/shard_map/ppermute | solution.py:91
  19.5 4.4 %copy-start.1 = (s32[4096]{0:T(1024)S(1)}, s32[4096]{0:T(1024)}, u32[]{:S(2)}) copy-start(s32[4096]{0:T(1024)} %param.7) | copy-start | bytes 49156
  19.5 21.5 %all-to-all-start = ((bf16[4,2,128,640]{3,2,1,0:T(8,128)(2,1)}), bf16[4,2,128,640]{3,2,1,0:T(8,128)(2,1)S(1)}, u32[]{:S(2)}, u32[]{:S(2)}) async-start(bf16[4,2,128,640]{3,2,1,0:T(8,128)(2,1)} %bitcast.1), calls=%async_computation | async-start | bytes 2621440 | tf_op jit(solution)/shard_map/all_to_all | solution.py:113
  25.1 1.6 %collective-permute-start.4 = (bf16[4,2,128,128]{3,2,1,0:T(8,128)(2,1)S(1)}, bf16[4,2,128,128]{3,2,1,0:T(8,128)(2,1)S(1)}, u32[]{:S(2)}, u32[]{:S(2)}) collective-permute-start(bf16[4,2,128,128]{3,2,1,0:T(8,128)(2,1)S(1)} %constant_dynamic-slice_fusion), channel_id=1, source_target_pairs={{0,8},{8,0},{16,24},{24,16},{32,40},{40,32},{48,56},{56,48},{64,72... | collective-permute-start | bytes 786440 | tf_op jit(solution)/shard_map/ppermute | solution.py:95
  56.0 1.5 %collective-permute-start.5 = (bf16[4,2,128,128]{3,2,1,0:T(8,128)(2,1)S(1)}, bf16[4,2,128,128]{3,2,1,0:T(8,128)(2,1)S(1)}, u32[]{:S(2)}, u32[]{:S(2)}) collective-permute-start(bf16[4,2,128,128]{3,2,1,0:T(8,128)(2,1)S(1)} %get-tuple-element.7), channel_id=1, source_target_pairs={{0,8},{8,0},{16,24},{24,16},{32,40},{40,32},{48,56},{56,48},{64,72... | collective-permute-start | bytes 786440 | tf_op jit(solution)/shard_map/ppermute | solution.py:95
  57.7 12.1 %collective-permute-start.6 = (bf16[2,128,128]{2,1,0:T(8,128)(2,1)S(1)}, bf16[2,128,128]{2,1,0:T(8,128)(2,1)S(1)}, u32[]{:S(2)}, u32[]{:S(2)}) collective-permute-start(bf16[2,128,128]{2,1,0:T(8,128)(2,1)S(1)} %get-tuple-element.16), channel_id=1, source_target_pairs={{64,0},{72,8},{80,16},{88,24},{96,32},{104,40},{112,48},{120,56},{... | collective-permute-start | bytes 196616 | tf_op jit(solution)/shard_map/ppermute | solution.py:91
  61.4 8.4 %collective-permute-start.9 = (bf16[2,128,128]{2,1,0:T(8,128)(2,1)S(1)}, bf16[2,128,128]{2,1,0:T(8,128)(2,1)S(1)}, u32[]{:S(2)}, u32[]{:S(2)}) collective-permute-start(bf16[2,128,128]{2,1,0:T(8,128)(2,1)S(1)} %get-tuple-element.17), channel_id=1, source_target_pairs={{16,0},{24,8},{32,16},{40,24},{48,32},{56,40},{64,48},{72,56},{80,... | collective-permute-start | bytes 196616 | tf_op jit(solution)/shard_map/ppermute | solution.py:91
  64.3 7.8 %collective-permute-start.8 = (bf16[2,128,128]{2,1,0:T(8,128)(2,1)S(1)}, bf16[2,128,128]{2,1,0:T(8,128)(2,1)S(1)}, u32[]{:S(2)}, u32[]{:S(2)}) collective-permute-start(bf16[2,128,128]{2,1,0:T(8,128)(2,1)S(1)} %get-tuple-element.18), channel_id=1, source_target_pairs={{32,0},{40,8},{48,16},{56,24},{64,32},{72,40},{80,48},{88,56},{96,... | collective-permute-start | bytes 196616 | tf_op jit(solution)/shard_map/ppermute | solution.py:91
  67.9 8.0 %collective-permute-start.7 = (bf16[2,128,128]{2,1,0:T(8,128)(2,1)S(1)}, bf16[2,128,128]{2,1,0:T(8,128)(2,1)S(1)}, u32[]{:S(2)}, u32[]{:S(2)}) collective-permute-start(bf16[2,128,128]{2,1,0:T(8,128)(2,1)S(1)} %get-tuple-element.19), channel_id=1, source_target_pairs={{48,0},{56,8},{64,16},{72,24},{80,32},{88,40},{96,48},{104,56},{11... | collective-permute-start | bytes 196616 | tf_op jit(solution)/shard_map/ppermute | solution.py:91
  92.9 12.2 %all-to-all-start.1 = ((bf16[4,128,640]{2,1,0:T(8,128)(2,1)}), bf16[4,128,640]{2,1,0:T(8,128)(2,1)S(1)}, u32[]{:S(2)}, u32[]{:S(2)}) async-start(bf16[4,128,640]{2,1,0:T(8,128)(2,1)} %get-tuple-element.5), calls=%async_computation.1 | async-start | bytes 1310720 | tf_op jit(solution)/shard_map/all_to_all | solution.py:141

commit v2 on v1

v2 whole, which is shorter than its diff:
```python
import functools, math
import jax, jax.numpy as jnp
from jax import lax
from jax.sharding import PartitionSpec as P
from jax.experimental import pallas as pl
from jax.experimental.pallas import tpu as pltpu


HD = 128
LINE = 4


def window_slots():
    core, chip = lax.axis_index("core"), lax.axis_index("z")
    turn = [lax.rem(i + LINE - chip, LINE) for i in range(LINE)]
    same = [2 * t for t in turn]
    cross = [lax.rem(2 * t + 1 + 6 * core, 2 * LINE) for t in turn]
    return chip, same, cross


def attn_kernel(slots, chunk, *refs):
    pieces, refs = refs[:slots], refs[slots:]
    line_ref, prev_ref, own_ref, cross_ref, bias_ref, *refs = refs
    dq_out, refs = refs[:slots], refs[slots:]
    dline, down, dcross, *refs = refs
    qd_ref, dq_ref, k_ref, v_ref, kt_ref, sc_ref, dp_ref, dsb_ref, dk_ref, dv_ref = refs
    tok, part = dq_out[0].shape
    groups = part // HD
    nkeys = k_ref.shape[0]
    scale = HD ** (-0.5)
    c2 = scale * math.log2(math.e)
    _, same_at, cross_at = window_slots()
    own_at = 2 * LINE

    def rows(w):
        return pl.ds(pl.multiple_of(w * tok, tok), tok)

    def put(w, kpart, vpart):
        k_ref[rows(w), :] = kpart
        v_ref[rows(w), :] = vpart
        kt_ref[:, rows(w)] = kpart.T

    for s in range(slots):
        qd_ref[s] = pieces[s][...]
    for i in range(LINE):
        put(same_at[i], line_ref[i, 0], line_ref[i, 1])
        put(cross_at[i], cross_ref[i, 0], cross_ref[i, 1])
    put(0, prev_ref[0], prev_ref[1])
    put(own_at, own_ref[0], own_ref[1])
    dk_ref[...] = jnp.zeros_like(dk_ref)
    dv_ref[...] = jnp.zeros_like(dv_ref)
    nt = (((1,), (1,)), ((), ()))
    wide = 2 * tok

    def folded(x):
        return x.reshape(chunk // 8, 8, wide)

    def step(p, carry):
        places = []
        for o in (0, 1):
            h = 2 * p + o
            slot = h // groups
            places.append((slot, pl.ds(pl.multiple_of((h - slot * groups) * HD, HD), HD)))
        (sa, na), (sb, nb_) = places
        qq = jnp.concatenate([qd_ref[sa, 0, :, na], qd_ref[sb, 0, :, nb_]], axis=0)
        dd = jnp.concatenate([qd_ref[sa, 1, :, na], qd_ref[sb, 1, :, nb_]], axis=0)
        top = jnp.full((8, wide), -3e38, jnp.float32)
        for c in range(0, nkeys, chunk):
            s = lax.dot_general(k_ref[c : c + chunk, :], qq, nt, preferred_element_type=jnp.float32)
            bias = bias_ref[c : c + chunk, :]
            s = s * c2 + jnp.concatenate([bias, bias], axis=1)
            sc_ref[c : c + chunk, :] = s
            top = jnp.maximum(top, jnp.max(folded(s), axis=0))
        top = jnp.max(top, axis=0, keepdims=True)
        tot = jnp.zeros((8, wide), jnp.float32)
        dl = jnp.zeros((8, wide), jnp.float32)
        for c in range(0, nkeys, chunk):
            dp = lax.dot_general(v_ref[c : c + chunk, :], dd, nt, preferred_element_type=jnp.float32)
            e = jnp.exp2(sc_ref[c : c + chunk, :] - top)
            tot = tot + jnp.sum(folded(e), axis=0)
            dl = dl + jnp.sum(folded(e * dp), axis=0)
            sc_ref[c : c + chunk, :] = e
            dp_ref[c : c + chunk, :] = dp
        rec = 1.0 / jnp.sum(tot, axis=0, keepdims=True)
        delta = jnp.sum(dl, axis=0, keepdims=True) * rec
        for c in range(0, nkeys, chunk):
            prob = (sc_ref[c : c + chunk, :] * rec).astype(jnp.bfloat16)
            ds = (prob.astype(jnp.float32) * (dp_ref[c : c + chunk, :] - delta)).astype(jnp.bfloat16)
            dsb_ref[c : c + chunk, :] = ds
            dv_ref[c : c + chunk, :] += jnp.dot(prob, dd, preferred_element_type=jnp.float32)
            dk_ref[c : c + chunk, :] += jnp.dot(ds, qq, preferred_element_type=jnp.float32)
        dqt = jnp.dot(kt_ref[...], dsb_ref[...], preferred_element_type=jnp.float32)
        dqq = (dqt.T * scale).astype(jnp.bfloat16)
        dq_ref[sa, :, na] = dqq[:tok]
        dq_ref[sb, :, nb_] = dqq[tok:]
        return carry

    lax.fori_loop(0, slots * groups // 2, step, 0)
    for s in range(slots):
        dq_out[s][...] = dq_ref[s]

    def grads(dst, w):
        dst[0] = (dk_ref[rows(w), :] * scale).astype(dst.dtype)
        dst[1] = dv_ref[rows(w), :].astype(dst.dtype)

    for i in range(LINE):
        grads(dline.at[i], same_at[i])
        grads(dcross.at[i], cross_at[i])
    grads(down, own_at)


def attn_parts(pieces, line, prev, own, cross, bias, chunk=384):
    slots = len(pieces)
    tok, part = pieces[0].shape[1:]
    nk = bias.shape[0]
    vm = pl.BlockSpec(memory_space=pltpu.VMEM)
    bf, f32 = jnp.bfloat16, jnp.float32
    return pl.pallas_call(
        functools.partial(attn_kernel, slots, chunk),
        out_shape=(
            *[jax.ShapeDtypeStruct((tok, part), bf) for _ in range(slots)],
            jax.ShapeDtypeStruct(line.shape, f32),
            jax.ShapeDtypeStruct(own.shape, f32),
            jax.ShapeDtypeStruct(cross.shape, bf),
        ),
        in_specs=[vm] * (slots + 5),
        out_specs=(vm,) * (slots + 3),
        scratch_shapes=[
            pltpu.VMEM((slots, 2, tok, part), bf),
            pltpu.VMEM((slots, tok, part), bf),
            pltpu.VMEM((nk, HD), bf),
            pltpu.VMEM((nk, HD), bf),
            pltpu.VMEM((HD, nk), bf),
            pltpu.VMEM((nk, 2 * tok), f32),
            pltpu.VMEM((nk, 2 * tok), f32),
            pltpu.VMEM((nk, 2 * tok), bf),
            pltpu.VMEM((nk, HD), f32),
            pltpu.VMEM((nk, HD), f32),
        ],
        cost_estimate=pl.CostEstimate(
            flops=10 * slots * tok * part * nk,
            bytes_accessed=4 * 1024 * 1024,
            transcendentals=slots * tok * part // HD * nk,
        ),
        compiler_params=pltpu.CompilerParams(vmem_limit_bytes=32 * 1024 * 1024),
        name="attn_bwd",
    )(*pieces, line, prev, own, cross, bias)


def join_kernel(sign, *refs):
    *pieces, out_ref, sems = refs
    count, part = len(pieces), pieces[0].shape[-1]
    head = lax.axis_index("x")
    copies = []
    for n, piece in enumerate(pieces):
        at = lax.rem(head + (count + sign * n) % count, count) * part
        copies.append(
            pltpu.make_async_copy(piece, out_ref.at[:, pl.ds(pl.multiple_of(at, HD), part)], sems.at[n])
        )
    for c in copies:
        c.start()
    for c in copies:
        c.wait()


def joined(pieces, sign):
    rows, part = pieces[0].shape
    vm = pl.BlockSpec(memory_space=pltpu.VMEM)
    return pl.pallas_call(
        functools.partial(join_kernel, sign),
        out_shape=jax.ShapeDtypeStruct((rows, len(pieces) * part), pieces[0].dtype),
        in_specs=[vm] * len(pieces),
        out_specs=pl.BlockSpec(memory_space=pl.ANY),
        scratch_shapes=[pltpu.SemaphoreType.DMA((len(pieces),))],
        compiler_params=pltpu.CompilerParams(vmem_limit_bytes=2 * 1024 * 1024),
        name="join_heads",
    )(*pieces)


def shifted(value, axis, steps, ring):
    count = lax.axis_size(axis)
    pairs = [(i, i + steps) for i in range(count)]
    pairs = [(i, j % count) for i, j in pairs if ring or 0 <= j < count]
    return lax.ppermute(value, axis, pairs)


def exchanged(value, axes):
    return lax.all_to_all(value, axes, 0, 0, tiled=True)


def chosen(which, options):
    out = options[0]
    for n, option in enumerate(options[1:], 1):
        out = jnp.where(which == n, option, out)
    return out


def body(queries, grad_out, keys_values, doc_ids):
    _, tok_rows, width = queries.shape
    kv_width = keys_values.shape[2]
    ring = lax.axis_size("x")
    part = width // ring
    core, chip, head = [lax.axis_index(a) for a in ("core", "z", "x")]
    place = (lax.axis_index("y") * LINE + chip) * 2 + core
    bf, f32 = jnp.bfloat16, jnp.float32
    chips = jnp.arange(LINE, dtype=jnp.int32).reshape(LINE, 1, 1, 1)

    def cut(arrays, k):
        at = lax.rem(head + k, ring) * part
        return jnp.stack([lax.dynamic_slice_in_dim(a[0], at, part, 1) for a in arrays])

    far = cut((queries, grad_out), 2)
    pieces = {2: shifted(far, "x", 2, True)}
    own = chosen(head, jnp.split(keys_values, ring, axis=2))
    prev = shifted(own, "y", 1, False)
    near = (queries, grad_out)
    for k in (1, 3):
        pieces[k] = shifted(cut(near, k), "x", k, True)
    pieces = [cut(near, 0), pieces[1], pieces[2], pieces[3]]
    line = exchanged(jnp.where(chips > chip, own[None], prev[None]), "z")
    cross = jnp.where(chips == chip, jnp.where(core == 1, prev, own)[None], line)
    cross = shifted(cross, "core", 1, True)

    total = (2 * LINE + 1) * tok_rows
    first = place * tok_rows
    qdoc = lax.dynamic_slice_in_dim(doc_ids, first, tok_rows, 0)
    padded = jnp.concatenate([jnp.full((total - tok_rows,), -1, jnp.int32), doc_ids])
    kdoc = lax.dynamic_slice_in_dim(padded, first, total, 0)
    kat = jnp.arange(total, dtype=jnp.int32) - (total - tok_rows)
    qat = jnp.arange(tok_rows, dtype=jnp.int32)
    seen = (kat[:, None] <= qat[None, :]) & (kdoc[:, None] == qdoc[None, :])
    bias = jnp.where(seen, 0.0, -1e30).astype(f32)

    *dq, dline, down, dcross = attn_parts(pieces, line, prev, own, cross, bias)

    arrived = shifted(dcross, "core", 1, True).astype(f32)
    dline = dline + jnp.where((chips != chip) | (core == 1), arrived, 0.0)
    later = shifted(jnp.where(chips >= chip, dline, 0.0).astype(bf), "y", -1, False)
    parts = [dq[0]] + [shifted(dq[k], "x", -k, True) for k in range(1, ring)]

    here = down[None] + jnp.where(core == 0, arrived, 0.0)
    later = later.astype(f32) + jnp.where(chips == chip, here, 0.0)
    grad = jnp.where(chips < chip, dline, later).astype(bf)
    sections = lax.axis_size("h") * ring
    rows = tok_rows // sections
    grad = grad.reshape(LINE, 2, sections, rows, HD).transpose(0, 2, 1, 3, 4)
    grad = exchanged(grad.reshape(LINE * sections, 2, rows, HD), ("z", "h", "x"))
    grad = grad.astype(f32).reshape(LINE * lax.axis_size("h"), ring, 2, rows, HD).sum(axis=0)
    grad_kv = grad.astype(bf).transpose(1, 2, 0, 3).reshape(2, rows, kv_width)
    grad_queries = joined(parts, 1).reshape(1, tok_rows, width)
    return (grad_queries, grad_kv)


def solution(mesh):
    names = ("y", "z", "core", "h", "x")
    fine = jax.sharding.Mesh(mesh.devices.reshape(-1, LINE, 2, 2, 4), names)
    ctx, section = names[:3], names[3:]
    return jax.shard_map(
        body,
        mesh=fine,
        in_specs=(P(section, ctx, None), P(section, ctx, None), P(None, ctx, None), P()),
        out_specs=(P(section, ctx, None), P(None, ctx + section, None)),
        check_vma=False,
    )
```

time: 107 us -> 83 us (0.78)
  the two profiles are of different devices: /device:TPU:16 before, /device:TPU:1 now
where the time goes in v2:
time: 83 us; the launch traced here: 82.6 us
  starting transfers between devices  31.7 us (38%)
  waiting for transfers between devices  29 us (35%)
  Pallas kernels  15.3 us (18%)
  local copies, waits for them, and re-layouts  3.85 us (5%)
  other arithmetic  1.97 us (2%)
  between operations  0.84 us (1%)
    ppermute x10, waiting for transfers between devices, shifted(): return lax.ppermute(value, axis, pairs)  24 us
    ppermute x10, starting transfers between devices, shifted(): return lax.ppermute(value, axis, pairs)  16.9 us
    all_to_all x2, starting transfers between devices, exchanged(): return lax.all_to_all(value, axes, 0, 0, tiled=True)  14.8 us
    pallas_call x1, Pallas kernels, attn_parts(): pl.pallas_call(functools.partial(attn_kernel, slots, chunk), out_shape=(*...  14.4 us
    all_to_all x2, waiting for transfers between devices, exchanged(): return lax.all_to_all(value, axes, 0, 0, tiled=True)  4.94 us
  transfers between devices with their start and end apart: 12, of which 8 were waited for; matrix products, arithmetic and copies ran while one was open for 2% of the time, Pallas kernels for 1%

profile of v2, /device:TPU:1, one launch (start us, length us, event | category | flops | bytes accessed | tf_op | source)
XLA Modules:
  0.0 82.6 jit_solution(8064820759855047262)
XLA Ops:
  0.7 1.5 %constant_dynamic-slice_fusion = (bf16[1,128,640]{2,1,0:T(8,128)(2,1)S(1)}, bf16[1,128,640]{2,1,0:T(8,128)(2,1)S(1)}, bf16[1,128,640]{2,1,0:T(8,128)(2,1)S(1)}, ...) fusion(bf16[1,128,2560]{2,1,0:T(8,128)(2,1)} %param.5, ...), kind=kLoop, calls=%fused_computation.23 | loop fusion | bytes 2621456 | tf_op jit(solution)/shard_map/dynamic_slice | solution.py:210
  2.2 3.4 %collective-permute-start.2 = (bf16[2,128,640]{2,1,0:T(8,128)(2,1)S(1)}, bf16[2,128,640]{2,1,0:T(8,128)(2,1)S(1)}, u32[]{:S(2)}, u32[]{:S(2)}) collective-permute-start(bf16[2,128,640]{2,1,0:T(8,128)(2,1)S(1)} %pad_maximum_fusion.3), channel_id=1, source_target_pairs={{0,3},{1,0},{2,1},{3,2},{4,7},{5,4},{6,5},{7,6},{8,11},{9,8},{10,9... | collective-permute-start | bytes 983048 | tf_op jit(solution)/shard_map/ppermute | solution.py:184
  5.6 0.6 collective-permute-start.1
  6.3 0.7 collective-permute-start
  7.0 0.2 copy-done
  7.2 3.2 %collective-permute-start.3 = (bf16[2,128,128]{2,1,0:T(8,128)(2,1)S(1)}, bf16[2,128,128]{2,1,0:T(8,128)(2,1)S(1)}, u32[]{:S(2)}, u32[]{:S(2)}) collective-permute-start(bf16[2,128,128]{2,1,0:T(8,128)(2,1)S(1)} %select_select_fusion.refs_6_), channel_id=1, source_target_pairs={{0,64},{64,128},{128,192},{1,65},{65,129},{129,193},{2,66},{66,130... | collective-permute-start | bytes 196616 | tf_op jit(solution)/shard_map/ppermute | solution.py:184
  10.5 1.3 %collective-permute-done.3.refs_5_ = bf16[2,128,128]{2,1,0:T(8,128)(2,1)S(1)} collective-permute-done((bf16[2,128,128]{2,1,0:T(8,128)(2,1)S(1)}, bf16[2,128,128]{2,1,0:T(8,128)(2,1)S(1)}, u32[]{:S(2)}, u32[]{:S(2)}) %collective-permute-start.3) | collective-permute-done | bytes 65568 | tf_op jit(solution)/shard_map/ppermute | solution.py:184
  11.7 0.8 broadcast_select_fusion.1
  12.5 5.6 %all-to-all-start = ((bf16[4,2,128,128]{3,2,1,0:T(8,128)(2,1)}), bf16[4,2,128,128]{3,2,1,0:T(8,128)(2,1)S(1)}, u32[]{:S(2)}, u32[]{:S(2)}) async-start(bf16[4,2,128,128]{3,2,1,0:T(8,128)(2,1)} %broadcast_select_fusion.1), calls=%async_computation | async-start | bytes 524288 | tf_op jit(solution)/shard_map/all_to_all | solution.py:188
  18.2 0.7 copy-done.1
  19.1 4.9 %all-to-all-done.refs_4_ = bf16[4,2,128,128]{3,2,1,0:T(8,128)(2,1)S(1)} async-done(((bf16[4,2,128,128]{3,2,1,0:T(8,128)(2,1)}), bf16[4,2,128,128]{3,2,1,0:T(8,128)(2,1)S(1)}, u32[]{:S(2)}, u32[]{:S(2)}) %all-to-all-start) | async-done | bytes 262176 | tf_op jit(solution)/shard_map/all_to_all | solution.py:188
  24.0 0.1 broadcast_select_fusion
  24.1 3.6 %collective-permute-start.4 = (bf16[4,2,128,128]{3,2,1,0:T(8,128)(2,1)S(1)}, bf16[4,2,128,128]{3,2,1,0:T(8,128)(2,1)S(1)}, u32[]{:S(2)}, u32[]{:S(2)}) collective-permute-start(bf16[4,2,128,128]{3,2,1,0:T(8,128)(2,1)S(1)} %broadcast_select_fusion), channel_id=1, source_target_pairs={{0,8},{8,0},{1,9},{9,1},{2,10},{10,2},{3,11},{11,3},{4,12},{12,4},... | collective-permute-start | bytes 786440 | tf_op jit(solution)/shard_map/ppermute | solution.py:184
  27.7 0.4 fusion.1.refs_8_
  28.1 0.7 collective-permute-done.4.refs_7_
  28.8 14.4 %attn_bwd.1 = (bf16[128,640]{1,0:T(8,128)(2,1)S(1)}, bf16[128,640]{1,0:T(8,128)(2,1)S(1)}, bf16[128,640]{1,0:T(8,128)(2,1)S(1)}, bf16[128,640]{1,0:T(8,128)(2,1)...) custom-call(bf16[2,128,640]{2,1,0:T(8,128)(2,1)S(1)} %pad_maximum_fusion.refs, ...), custom_call_target="tpu_custom_call" | custom-call | flops 3774873600 | bytes 4194304 | tf_op jit(solution)/shard_map/attn_bwd/pallas_call | solution.py:118
  43.3 0.5 collective-permute-start.8
  43.7 1.2 %collective-permute-done.8 = bf16[4,2,128,128]{3,2,1,0:T(8,128)(2,1)S(1)} collective-permute-done((bf16[4,2,128,128]{3,2,1,0:T(8,128)(2,1)S(1)}, bf16[4,2,128,128]{3,2,1,0:T(8,128)(2,1)S(1)}, u32[]{:S(2)}, u32[]{:S(2)}) %collective-permute-start.8) | collective-permute-done | bytes 262176 | tf_op jit(solution)/shard_map/ppermute | solution.py:184
  44.9 0.2 select_convert_fusion
  45.1 1.3 %collective-permute-start.9 = (bf16[4,2,128,128]{3,2,1,0:T(8,128)(2,1)S(1)}, bf16[4,2,128,128]{3,2,1,0:T(8,128)(2,1)S(1)}, u32[]{:S(2)}, u32[]{:S(2)}) collective-permute-start(bf16[4,2,128,128]{3,2,1,0:T(8,128)(2,1)S(1)} %select_convert_fusion), channel_id=1, source_target_pairs={{64,0},{128,64},{192,128},{65,1},{129,65},{193,129},{66,2},{130,66... | collective-permute-start | bytes 786440 | tf_op jit(solution)/shard_map/ppermute | solution.py:184
  46.4 9.0 %collective-permute-done.9 = bf16[4,2,128,128]{3,2,1,0:T(8,128)(2,1)S(1)} collective-permute-done((bf16[4,2,128,128]{3,2,1,0:T(8,128)(2,1)S(1)}, bf16[4,2,128,128]{3,2,1,0:T(8,128)(2,1)S(1)}, u32[]{:S(2)}, u32[]{:S(2)}) %collective-permute-start.9) | collective-permute-done | bytes 262176 | tf_op jit(solution)/shard_map/ppermute | solution.py:184
  55.3 0.2 fusion.7
  55.6 0.7 copy.8
  56.3 9.2 %all-to-all-start.1 = ((bf16[32,2,16,128]{3,2,1,0:T(8,128)(2,1)}), bf16[32,2,16,128]{3,2,1,0:T(8,128)(2,1)S(1)}, u32[]{:S(2)}, u32[]{:S(2)}) async-start(bf16[32,2,16,128]{3,2,1,0:T(8,128)(2,1)} %bitcast.3), calls=%async_computation.1 | async-start | bytes 524288 | tf_op jit(solution)/shard_map/all_to_all | solution.py:188
  65.5 2.5 %collective-permute-start.5 = (bf16[128,640]{1,0:T(8,128)(2,1)S(1)}, bf16[128,640]{1,0:T(8,128)(2,1)S(1)}, u32[]{:S(2)}, u32[]{:S(2)}) collective-permute-start(bf16[128,640]{1,0:T(8,128)(2,1)S(1)} %get-tuple-element.10), channel_id=1, source_target_pairs={{0,3},{1,0},{2,1},{3,2},{4,7},{5,4},{6,5},{7,6},{8,11},{9,8},{10,9... | collective-permute-start | bytes 491528 | tf_op jit(solution)/shard_map/ppermute | solution.py:184
  68.0 0.6 collective-permute-start.6
  68.6 0.6 collective-permute-start.7
  69.2 5.4 %collective-permute-done.5.refs_1_ = bf16[128,640]{1,0:T(8,128)(2,1)S(1)} collective-permute-done((bf16[128,640]{1,0:T(8,128)(2,1)S(1)}, bf16[128,640]{1,0:T(8,128)(2,1)S(1)}, u32[]{:S(2)}, u32[]{:S(2)}) %collective-permute-start.5) | collective-permute-done | bytes 163872 | tf_op jit(solution)/shard_map/ppermute | solution.py:184
  74.6 1.8 %collective-permute-done.6.refs_2_ = bf16[128,640]{1,0:T(8,128)(2,1)S(1)} collective-permute-done((bf16[128,640]{1,0:T(8,128)(2,1)S(1)}, bf16[128,640]{1,0:T(8,128)(2,1)S(1)}, u32[]{:S(2)}, u32[]{:S(2)}) %collective-permute-start.6) | collective-permute-done | bytes 163872 | tf_op jit(solution)/shard_map/ppermute | solution.py:184
  76.4 4.7 %collective-permute-done.7.refs_3_ = bf16[128,640]{1,0:T(8,128)(2,1)S(1)} collective-permute-done((bf16[128,640]{1,0:T(8,128)(2,1)S(1)}, bf16[128,640]{1,0:T(8,128)(2,1)S(1)}, u32[]{:S(2)}, u32[]{:S(2)}) %collective-permute-start.7) | collective-permute-done | bytes 163872 | tf_op jit(solution)/shard_map/ppermute | solution.py:184
  81.1 0.9 %join_heads.1 = bf16[128,2560]{1,0:T(8,128)(2,1)} custom-call(bf16[128,640]{1,0:T(8,128)(2,1)S(1)} %get-tuple-element.9.refs_0_, bf16[128,640]{1,0:T(8,128)(2,1)S(1)} %collective-permute-done.5.refs_1_, bf16[128,640]{1,0:T(8,128)(2,1)S(1)} %collective-permute-done.6.refs_2_, bf16[128,640]{1,0:T(8,128)(2,1)S(1)} %collective-permute-done.7.refs_3_), custom_call_target="tpu_custom_call" | custom-call | tf_op jit(solution)/shard_map/join_heads/pallas_call | solution.py:169
  82.0 0.6 copy_bitcast_fusion
  (19 shorter events, 0.4 us)
Async XLA Ops:
  2.2 25.8 %collective-permute-start.2 = (bf16[2,128,640]{2,1,0:T(8,128)(2,1)S(1)}, bf16[2,128,640]{2,1,0:T(8,128)(2,1)S(1)}, u32[]{:S(2)}, u32[]{:S(2)}) collective-permute-start(bf16[2,128,640]{2,1,0:T(8,128)(2,1)S(1)} %pad_maximum_fusion.3), channel_id=1, source_target_pairs={{0,3},{1,0},{2,1},{3,2},{4,7},{5,4},{6,5},{7,6},{8,11},{9,8},{10,9... | collective-permute-start | bytes 983048 | tf_op jit(solution)/shard_map/ppermute | solution.py:184
  5.6 22.4 %collective-permute-start.1 = (bf16[2,128,640]{2,1,0:T(8,128)(2,1)S(1)}, bf16[2,128,640]{2,1,0:T(8,128)(2,1)S(1)}, u32[]{:S(2)}, u32[]{:S(2)}) collective-permute-start(bf16[2,128,640]{2,1,0:T(8,128)(2,1)S(1)} %pad_maximum_fusion.2), channel_id=1, source_target_pairs={{0,2},{1,3},{2,0},{3,1},{4,6},{5,7},{6,4},{7,5},{8,10},{9,11},{10,... | collective-permute-start | bytes 983048 | tf_op jit(solution)/shard_map/ppermute | solution.py:184
  6.3 0.9 %copy-start = (bf16[2,128,512]{2,1,0:T(8,128)(2,1)S(1)}, bf16[2,128,512]{2,1,0:T(8,128)(2,1)}, u32[]{:S(2)}) copy-start(bf16[2,128,512]{2,1,0:T(8,128)(2,1)} %param.6) | copy-start | bytes 786436
  6.3 21.8 %collective-permute-start = (bf16[2,128,640]{2,1,0:T(8,128)(2,1)S(1)}, bf16[2,128,640]{2,1,0:T(8,128)(2,1)S(1)}, u32[]{:S(2)}, u32[]{:S(2)}) collective-permute-start(bf16[2,128,640]{2,1,0:T(8,128)(2,1)S(1)} %pad_maximum_fusion.1), channel_id=1, source_target_pairs={{0,1},{1,2},{2,3},{3,0},{4,5},{5,6},{6,7},{7,4},{8,9},{9,10},{10,1... | collective-permute-start | bytes 983048 | tf_op jit(solution)/shard_map/ppermute | solution.py:184
  7.2 4.5 %collective-permute-start.3 = (bf16[2,128,128]{2,1,0:T(8,128)(2,1)S(1)}, bf16[2,128,128]{2,1,0:T(8,128)(2,1)S(1)}, u32[]{:S(2)}, u32[]{:S(2)}) collective-permute-start(bf16[2,128,128]{2,1,0:T(8,128)(2,1)S(1)} %select_select_fusion.refs_6_), channel_id=1, source_target_pairs={{0,64},{64,128},{128,192},{1,65},{65,129},{129,193},{2,66},{66,130... | collective-permute-start | bytes 196616 | tf_op jit(solution)/shard_map/ppermute | solution.py:184
  12.5 11.5 %all-to-all-start = ((bf16[4,2,128,128]{3,2,1,0:T(8,128)(2,1)}), bf16[4,2,128,128]{3,2,1,0:T(8,128)(2,1)S(1)}, u32[]{:S(2)}, u32[]{:S(2)}) async-start(bf16[4,2,128,128]{3,2,1,0:T(8,128)(2,1)} %broadcast_select_fusion.1), calls=%async_computation | async-start | bytes 524288 | tf_op jit(solution)/shard_map/all_to_all | solution.py:188
  18.2 0.7 copy-start.1
  24.1 4.7 %collective-permute-start.4 = (bf16[4,2,128,128]{3,2,1,0:T(8,128)(2,1)S(1)}, bf16[4,2,128,128]{3,2,1,0:T(8,128)(2,1)S(1)}, u32[]{:S(2)}, u32[]{:S(2)}) collective-permute-start(bf16[4,2,128,128]{3,2,1,0:T(8,128)(2,1)S(1)} %broadcast_select_fusion), channel_id=1, source_target_pairs={{0,8},{8,0},{1,9},{9,1},{2,10},{10,2},{3,11},{11,3},{4,12},{12,4},... | collective-permute-start | bytes 786440 | tf_op jit(solution)/shard_map/ppermute | solution.py:184
  43.3 1.6 %collective-permute-start.8 = (bf16[4,2,128,128]{3,2,1,0:T(8,128)(2,1)S(1)}, bf16[4,2,128,128]{3,2,1,0:T(8,128)(2,1)S(1)}, u32[]{:S(2)}, u32[]{:S(2)}) collective-permute-start(bf16[4,2,128,128]{3,2,1,0:T(8,128)(2,1)S(1)} %get-tuple-element.14), channel_id=1, source_target_pairs={{0,8},{8,0},{1,9},{9,1},{2,10},{10,2},{3,11},{11,3},{4,12},{12,4},... | collective-permute-start | bytes 786440 | tf_op jit(solution)/shard_map/ppermute | solution.py:184
  45.1 10.3 %collective-permute-start.9 = (bf16[4,2,128,128]{3,2,1,0:T(8,128)(2,1)S(1)}, bf16[4,2,128,128]{3,2,1,0:T(8,128)(2,1)S(1)}, u32[]{:S(2)}, u32[]{:S(2)}) collective-permute-start(bf16[4,2,128,128]{3,2,1,0:T(8,128)(2,1)S(1)} %select_convert_fusion), channel_id=1, source_target_pairs={{64,0},{128,64},{192,128},{65,1},{129,65},{193,129},{66,2},{130,66... | collective-permute-start | bytes 786440 | tf_op jit(solution)/shard_map/ppermute | solution.py:184
  56.3 25.7 %all-to-all-start.1 = ((bf16[32,2,16,128]{3,2,1,0:T(8,128)(2,1)}), bf16[32,2,16,128]{3,2,1,0:T(8,128)(2,1)S(1)}, u32[]{:S(2)}, u32[]{:S(2)}) async-start(bf16[32,2,16,128]{3,2,1,0:T(8,128)(2,1)} %bitcast.3), calls=%async_computation.1 | async-start | bytes 524288 | tf_op jit(solution)/shard_map/all_to_all | solution.py:188
  65.5 9.1 %collective-permute-start.5 = (bf16[128,640]{1,0:T(8,128)(2,1)S(1)}, bf16[128,640]{1,0:T(8,128)(2,1)S(1)}, u32[]{:S(2)}, u32[]{:S(2)}) collective-permute-start(bf16[128,640]{1,0:T(8,128)(2,1)S(1)} %get-tuple-element.10), channel_id=1, source_target_pairs={{0,3},{1,0},{2,1},{3,2},{4,7},{5,4},{6,5},{7,6},{8,11},{9,8},{10,9... | collective-permute-start | bytes 491528 | tf_op jit(solution)/shard_map/ppermute | solution.py:184
  68.0 8.4 %collective-permute-start.6 = (bf16[128,640]{1,0:T(8,128)(2,1)S(1)}, bf16[128,640]{1,0:T(8,128)(2,1)S(1)}, u32[]{:S(2)}, u32[]{:S(2)}) collective-permute-start(bf16[128,640]{1,0:T(8,128)(2,1)S(1)} %get-tuple-element.11), channel_id=1, source_target_pairs={{0,2},{1,3},{2,0},{3,1},{4,6},{5,7},{6,4},{7,5},{8,10},{9,11},{10,... | collective-permute-start | bytes 491528 | tf_op jit(solution)/shard_map/ppermute | solution.py:184
  68.6 12.5 %collective-permute-start.7 = (bf16[128,640]{1,0:T(8,128)(2,1)S(1)}, bf16[128,640]{1,0:T(8,128)(2,1)S(1)}, u32[]{:S(2)}, u32[]{:S(2)}) collective-permute-start(bf16[128,640]{1,0:T(8,128)(2,1)S(1)} %get-tuple-element.12), channel_id=1, source_target_pairs={{0,1},{1,2},{2,3},{3,0},{4,5},{5,6},{6,7},{7,4},{8,9},{9,10},{10,1... | collective-permute-start | bytes 491528 | tf_op jit(solution)/shard_map/ppermute | solution.py:184

commit v3 on v2

--- a/solution.py
+++ b/solution.py
@@ -18,13 +18,20 @@
     return chip, same, cross
 
 
+def head_places(pair, groups):
+    places = []
+    for h in (2 * pair, 2 * pair + 1):
+        slot = h // groups
+        places.append((slot, pl.ds(pl.multiple_of((h - slot * groups) * HD, HD), HD)))
+    return places
+
+
 def attn_kernel(slots, chunk, *refs):
     pieces, refs = refs[:slots], refs[slots:]
     line_ref, prev_ref, own_ref, cross_ref, bias_ref, *refs = refs
-    dq_out, refs = refs[:slots], refs[slots:]
-    dline, down, dcross, *refs = refs
-    qd_ref, dq_ref, k_ref, v_ref, kt_ref, sc_ref, dp_ref, dsb_ref, dk_ref, dv_ref = refs
-    tok, part = dq_out[0].shape
+    ds_ref, kt_ref, dline, down, dcross, *refs = refs
+    qd_ref, k_ref, v_ref, dk_ref, dv_ref, *pairs = refs
+    tok, part = pieces[0].shape[1:]
     groups = part // HD
     nkeys = k_ref.shape[0]
     scale = HD ** (-0.5)
@@ -55,12 +62,8 @@
     def folded(x):
         return x.reshape(chunk // 8, 8, wide)
 
-    def step(p, carry):
-        places = []
-        for o in (0, 1):
-            h = 2 * p + o
-            slot = h // groups
-            places.append((slot, pl.ds(pl.multiple_of((h - slot * groups) * HD, HD), HD)))
+    def one(p, sc_ref, dp_ref):
+        places = head_places(p, groups)
         (sa, na), (sb, nb_) = places
         qq = jnp.concatenate([qd_ref[sa, 0, :, na], qd_ref[sb, 0, :, nb_]], axis=0)
         dd = jnp.concatenate([qd_ref[sa, 1, :, na], qd_ref[sb, 1, :, nb_]], axis=0)
@@ -86,22 +89,21 @@
         for c in range(0, nkeys, chunk):
             prob = (sc_ref[c : c + chunk, :] * rec).astype(jnp.bfloat16)
             ds = (prob.astype(jnp.float32) * (dp_ref[c : c + chunk, :] - delta)).astype(jnp.bfloat16)
-            dsb_ref[c : c + chunk, :] = ds
+            ds_ref[p, c : c + chunk, :] = ds
             dv_ref[c : c + chunk, :] += jnp.dot(prob, dd, preferred_element_type=jnp.float32)
             dk_ref[c : c + chunk, :] += jnp.dot(ds, qq, preferred_element_type=jnp.float32)
-        dqt = jnp.dot(kt_ref[...], dsb_ref[...], preferred_element_type=jnp.float32)
-        dqq = (dqt.T * scale).astype(jnp.bfloat16)
-        dq_ref[sa, :, na] = dqq[:tok]
-        dq_ref[sb, :, nb_] = dqq[tok:]
+
+    def step(t, carry):
+        for u in range(2):
+            one(2 * t + u, pairs[2 * u], pairs[2 * u + 1])
         return carry
 
-    lax.fori_loop(0, slots * groups // 2, step, 0)
-    for s in range(slots):
-        dq_out[s][...] = dq_ref[s]
+    lax.fori_loop(0, slots * groups // 4, step, 0)
 
     def grads(dst, w):
-        dst[0] = (dk_ref[rows(w), :] * scale).astype(dst.dtype)
-        dst[1] = dv_ref[rows(w), :].astype(dst.dtype)
+        block = (dst.shape[0], dst.shape[2], HD)
+        dst[:, 0] = (dk_ref[rows(w), :] * scale).astype(dst.dtype).reshape(block)
+        dst[:, 1] = dv_ref[rows(w), :].astype(dst.dtype).reshape(block)
 
     for i in range(LINE):
         grads(dline.at[i], same_at[i])
@@ -109,42 +111,76 @@
     grads(down, own_at)
 
 
-def attn_parts(pieces, line, prev, own, cross, bias, chunk=384):
+def attn_parts(pieces, line, prev, own, cross, bias, sections, chunk=384):
     slots = len(pieces)
     tok, part = pieces[0].shape[1:]
     nk = bias.shape[0]
+    block = (sections, 2, tok // sections, HD)
     vm = pl.BlockSpec(memory_space=pltpu.VMEM)
     bf, f32 = jnp.bfloat16, jnp.float32
     return pl.pallas_call(
         functools.partial(attn_kernel, slots, chunk),
         out_shape=(
-            *[jax.ShapeDtypeStruct((tok, part), bf) for _ in range(slots)],
-            jax.ShapeDtypeStruct(line.shape, f32),
-            jax.ShapeDtypeStruct(own.shape, f32),
-            jax.ShapeDtypeStruct(cross.shape, bf),
+            jax.ShapeDtypeStruct((slots * part // HD // 2, nk, 2 * tok), bf),
+            jax.ShapeDtypeStruct((HD, nk), bf),
+            jax.ShapeDtypeStruct((LINE,) + block, f32),
+            jax.ShapeDtypeStruct(block, f32),
+            jax.ShapeDtypeStruct((LINE,) + block, bf),
         ),
         in_specs=[vm] * (slots + 5),
-        out_specs=(vm,) * (slots + 3),
+        out_specs=(vm,) * 5,
         scratch_shapes=[
             pltpu.VMEM((slots, 2, tok, part), bf),
-            pltpu.VMEM((slots, tok, part), bf),
             pltpu.VMEM((nk, HD), bf),
             pltpu.VMEM((nk, HD), bf),
-            pltpu.VMEM((HD, nk), bf),
-            pltpu.VMEM((nk, 2 * tok), f32),
-            pltpu.VMEM((nk, 2 * tok), f32),
-            pltpu.VMEM((nk, 2 * tok), bf),
             pltpu.VMEM((nk, HD), f32),
             pltpu.VMEM((nk, HD), f32),
+            *[pltpu.VMEM((nk, 2 * tok), f32) for _ in range(4)],
         ],
         cost_estimate=pl.CostEstimate(
-            flops=10 * slots * tok * part * nk,
+            flops=8 * slots * tok * part * nk,
             bytes_accessed=4 * 1024 * 1024,
             transcendentals=slots * tok * part // HD * nk,
         ),
-        compiler_params=pltpu.CompilerParams(vmem_limit_bytes=32 * 1024 * 1024),
+        compiler_params=pltpu.CompilerParams(vmem_limit_bytes=24 * 1024 * 1024),
         name="attn_bwd",
     )(*pieces, line, prev, own, cross, bias)
+
+
+def dq_kernel(slots, ds_ref, kt_ref, *refs):
+    dq_out, dq_ref = refs[:slots], refs[slots]
+    tok, part = dq_out[0].shape
+    scale = HD ** (-0.5)
+
+    def step(t, carry):
+        for u in range(2):
+            p = 2 * t + u
+            dqt = jnp.dot(kt_ref[...], ds_ref[p], preferred_element_type=jnp.float32)
+            dqq = (dqt.T * scale).astype(jnp.bfloat16)
+            for o, (slot, n) in enumerate(head_places(p, part // HD)):
+                dq_ref[slot, :, n] = dqq[o * tok : (o + 1) * tok]
+        return carry
+
+    lax.fori_loop(0, ds_ref.shape[0] // 2, step, 0)
+    for s in range(slots):
+        dq_out[s][...] = dq_ref[s]
+
+
+def dq_parts(ds, kt, slots, tok, part):
+    vm = pl.BlockSpec(memory_space=pltpu.VMEM)
+    bf = jnp.bfloat16
+    return pl.pallas_call(
+        functools.partial(dq_kernel, slots),
+        out_shape=tuple(jax.ShapeDtypeStruct((tok, part), bf) for _ in range(slots)),
+        in_specs=[vm] * 2,
+        out_specs=(vm,) * slots,
+        scratch_shapes=[pltpu.VMEM((slots, tok, part), bf)],
+        cost_estimate=pl.CostEstimate(
+            flops=2 * ds.size * HD, bytes_accessed=2 * ds.size, transcendentals=0
+        ),
+        compiler_params=pltpu.CompilerParams(vmem_limit_bytes=12 * 1024 * 1024),
+        name="attn_dq",
+    )(ds, kt)
 
 
 def join_kernel(sign, *refs):
@@ -231,19 +267,20 @@
     seen = (kat[:, None] <= qat[None, :]) & (kdoc[:, None] == qdoc[None, :])
     bias = jnp.where(seen, 0.0, -1e30).astype(f32)
 
-    *dq, dline, down, dcross = attn_parts(pieces, line, prev, own, cross, bias)
+    sections = lax.axis_size("h") * ring
+    ds, kt, dline, down, dcross = attn_parts(pieces, line, prev, own, cross, bias, sections)
 
     arrived = shifted(dcross, "core", 1, True).astype(f32)
+    chips = chips[..., None]
     dline = dline + jnp.where((chips != chip) | (core == 1), arrived, 0.0)
     later = shifted(jnp.where(chips >= chip, dline, 0.0).astype(bf), "y", -1, False)
+    dq = dq_parts(ds, kt, ring, tok_rows, part)
     parts = [dq[0]] + [shifted(dq[k], "x", -k, True) for k in range(1, ring)]
 
-    here = down[None] + jnp.where(core == 0, arrived, 0.0)
+    here = down[None] + jnp.where(core == 1, 0.0, arrived)
     later = later.astype(f32) + jnp.where(chips == chip, here, 0.0)
     grad = jnp.where(chips < chip, dline, later).astype(bf)
-    sections = lax.axis_size("h") * ring
     rows = tok_rows // sections
-    grad = grad.reshape(LINE, 2, sections, rows, HD).transpose(0, 2, 1, 3, 4)
     grad = exchanged(grad.reshape(LINE * sections, 2, rows, HD), ("z", "h", "x"))
     grad = grad.astype(f32).reshape(LINE * lax.axis_size("h"), ring, 2, rows, HD).sum(axis=0)
     grad_kv = grad.astype(bf).transpose(1, 2, 0, 3).reshape(2, rows, kv_width)

time: 83 us -> 86 us (1.036)
  local copies, waits for them, and re-layouts: 3.85 us -> 7.45 us
  waiting for transfers between devices: 29 us -> 27.3 us
  other arithmetic: 1.97 us -> 3.6 us
    unnamed x4 -> x8, local copies, waits for them, and re-layouts: 0.93 us -> 5.21 us
    ppermute x10, waiting for transfers between devices: 24 us -> 21.9 us  [shifted(): return lax.ppermute(value, axis, pairs)]
    select_n x1, other arithmetic: 0.02 us -> 0.96 us  [chosen(): out = jnp.where(which == n, option, out)]
    pallas_call x1 -> x2, Pallas kernels: 14.4 us -> 14.3 us  [the longest x1 12 us: attn_parts(): pl.pallas_call(functools.partial(attn_kernel, slots, chunk), out_shape=(j...]
  transfers between devices with their start and end apart: 12 -> 12, of which waited for: 8 -> 8; matrix products, arithmetic and copies ran while one was open for 2% -> 3% of each run, Pallas kernels for 1% -> 4%
where the time goes in v3:
time: 86 us; the launch traced here: 85.6 us
  starting transfers between devices  31.3 us (36%)
  waiting for transfers between devices  27.3 us (32%)
  Pallas kernels  15.1 us (18%)
  local copies, waits for them, and re-layouts  7.45 us (9%)
  other arithmetic  3.6 us (4%)
  between operations  0.86 us (1%)
    ppermute x10, waiting for transfers between devices, shifted(): return lax.ppermute(value, axis, pairs)  21.9 us
    ppermute x10, starting transfers between devices, shifted(): return lax.ppermute(value, axis, pairs)  17.1 us
    all_to_all x2, starting transfers between devices, exchanged(): return lax.all_to_all(value, axes, 0, 0, tiled=True)  14.2 us
    pallas_call x1, Pallas kernels, attn_parts(): pl.pallas_call(functools.partial(attn_kernel, slots, chunk), out_shape=(j...  12 us
    all_to_all x2, waiting for transfers between devices, exchanged(): return lax.all_to_all(value, axes, 0, 0, tiled=True)  5.43 us
    unnamed x8, local copies, waits for them, and re-layouts  5.21 us
    pallas_call x1, Pallas kernels, dq_parts(): pl.pallas_call(functools.partial(dq_kernel, slots), out_shape=tuple((jax....  2.31 us
  transfers between devices with their start and end apart: 12, of which 8 were waited for; matrix products, arithmetic and copies ran while one was open for 3% of the time, Pallas kernels for 4%

profile of v3, /device:TPU:1, one launch (start us, length us, event | category | flops | bytes accessed | tf_op | source)
XLA Modules:
  0.0 85.6 jit_solution(4451655894257476595)
XLA Ops:
  0.7 1.5 %constant_dynamic-slice_fusion = (bf16[1,128,640]{2,1,0:T(8,128)(2,1)S(1)}, bf16[1,128,640]{2,1,0:T(8,128)(2,1)S(1)}, bf16[1,128,640]{2,1,0:T(8,128)(2,1)S(1)}, ...) fusion(bf16[1,128,2560]{2,1,0:T(8,128)(2,1)} %param.5, ...), kind=kLoop, calls=%fused_computation.23 | loop fusion | bytes 2621456 | tf_op jit(solution)/shard_map/dynamic_slice | solution.py:246
  2.3 3.4 %collective-permute-start.2 = (bf16[2,128,640]{2,1,0:T(8,128)(2,1)S(1)}, bf16[2,128,640]{2,1,0:T(8,128)(2,1)S(1)}, u32[]{:S(2)}, u32[]{:S(2)}) collective-permute-start(bf16[2,128,640]{2,1,0:T(8,128)(2,1)S(1)} %pad_maximum_fusion.3), channel_id=1, source_target_pairs={{0,3},{1,0},{2,1},{3,2},{4,7},{5,4},{6,5},{7,6},{8,11},{9,8},{10,9... | collective-permute-start | bytes 983048 | tf_op jit(solution)/shard_map/ppermute | solution.py:220
  5.7 0.6 collective-permute-start.1
  6.3 0.7 collective-permute-start
  7.0 1.0 %select_select_fusion.refs_6_ = bf16[2,128,128]{2,1,0:T(8,128)(2,1)S(1)} fusion(bf16[2,128,512]{2,1,0:T(8,128)(2,1)} %param.6, pred[]{:T(512)S(6)} %eq.45, pred[]{:T(512)S(6)} %eq.44, pred[]{:T(512)S(6)} %eq.43), kind=kLoop, calls=%fused_computation.18 | loop fusion | flops 98304 | bytes 327683 | tf_op jit(solution)/shard_map/jit(_where)/select_n | solution.py:230
  8.0 3.2 %collective-permute-start.3 = (bf16[2,128,128]{2,1,0:T(8,128)(2,1)S(1)}, bf16[2,128,128]{2,1,0:T(8,128)(2,1)S(1)}, u32[]{:S(2)}, u32[]{:S(2)}) collective-permute-start(bf16[2,128,128]{2,1,0:T(8,128)(2,1)S(1)} %select_select_fusion.refs_6_), channel_id=1, source_target_pairs={{0,64},{64,128},{128,192},{1,65},{65,129},{129,193},{2,66},{66,130... | collective-permute-start | bytes 196616 | tf_op jit(solution)/shard_map/ppermute | solution.py:220
  11.2 1.3 %collective-permute-done.3.refs_5_ = bf16[2,128,128]{2,1,0:T(8,128)(2,1)S(1)} collective-permute-done((bf16[2,128,128]{2,1,0:T(8,128)(2,1)S(1)}, bf16[2,128,128]{2,1,0:T(8,128)(2,1)S(1)}, u32[]{:S(2)}, u32[]{:S(2)}) %collective-permute-start.3) | collective-permute-done | bytes 65568 | tf_op jit(solution)/shard_map/ppermute | solution.py:220
  12.5 0.8 broadcast_select_fusion.1
  13.3 5.6 %all-to-all-start = ((bf16[4,2,128,128]{3,2,1,0:T(8,128)(2,1)}), bf16[4,2,128,128]{3,2,1,0:T(8,128)(2,1)S(1)}, u32[]{:S(2)}, u32[]{:S(2)}) async-start(bf16[4,2,128,128]{3,2,1,0:T(8,128)(2,1)} %broadcast_select_fusion.1), calls=%async_computation | async-start | bytes 524288 | tf_op jit(solution)/shard_map/all_to_all | solution.py:224
  19.1 5.4 %all-to-all-done.refs_4_ = bf16[4,2,128,128]{3,2,1,0:T(8,128)(2,1)S(1)} async-done(((bf16[4,2,128,128]{3,2,1,0:T(8,128)(2,1)}), bf16[4,2,128,128]{3,2,1,0:T(8,128)(2,1)S(1)}, u32[]{:S(2)}, u32[]{:S(2)}) %all-to-all-start) | async-done | bytes 262176 | tf_op jit(solution)/shard_map/all_to_all | solution.py:224
  24.6 3.9 %collective-permute-start.4 = (bf16[4,2,128,128]{3,2,1,0:T(8,128)(2,1)S(1)}, bf16[4,2,128,128]{3,2,1,0:T(8,128)(2,1)S(1)}, u32[]{:S(2)}, u32[]{:S(2)}) collective-permute-start(bf16[4,2,128,128]{3,2,1,0:T(8,128)(2,1)S(1)} %broadcast_select_fusion), channel_id=1, source_target_pairs={{0,8},{8,0},{1,9},{9,1},{2,10},{10,2},{3,11},{11,3},{4,12},{12,4},... | collective-permute-start | bytes 786440 | tf_op jit(solution)/shard_map/ppermute | solution.py:220
  28.5 0.4 fusion.1.refs_8_
  29.0 0.7 collective-permute-done.4.refs_7_
  29.7 12.0 %attn_bwd.1 = (bf16[10,1152,256]{2,1,0:T(8,128)(2,1)S(1)}, bf16[128,1152]{1,0:T(8,128)(2,1)S(1)}, f32[4,8,2,16,128]{4,3,2,1,0:T(8,128)S(1)}, f32[8,2,16,128]{3,2...) custom-call(bf16[2,128,640]{2,1,0:T(8,128)(2,1)S(1)} %pad_maximum_fusion.refs_0_, ...), custom_call_target="tpu_custom_call" | custom-call | flops 3019898880 | bytes 4194304 | tf_op jit(solution)/shard_map/attn_bwd/pallas_call | solution.py:121
  41.7 2.5 %copy-done = bf16[10,1152,256]{2,1,0:T(8,128)(2,1)} copy-done((bf16[10,1152,256]{2,1,0:T(8,128)(2,1)}, bf16[10,1152,256]{2,1,0:T(8,128)(2,1)S(1)}, u32[]{:S(2)}) %copy-start) | copy-done | bytes 5898264
  44.2 0.4 collective-permute-start.8
  44.6 1.2 %collective-permute-done.8 = bf16[4,8,2,16,128]{4,3,2,1,0:T(8,128)(2,1)S(1)} collective-permute-done((bf16[4,8,2,16,128]{4,3,2,1,0:T(8,128)(2,1)S(1)}, bf16[4,8,2,16,128]{4,3,2,1,0:T(8,128)(2,1)S(1)}, u32[]{:S(2)}, u32[]{:S(2)}) %collective-permute-start.8) | collective-permute-done | bytes 262176 | tf_op jit(solution)/shard_map/ppermute | solution.py:220
  45.8 0.2 select_convert_fusion
  45.9 1.3 %collective-permute-start.9 = (bf16[4,8,2,16,128]{4,3,2,1,0:T(8,128)(2,1)S(1)}, bf16[4,8,2,16,128]{4,3,2,1,0:T(8,128)(2,1)S(1)}, u32[]{:S(2)}, u32[]{:S(2)}) collective-permute-start(bf16[4,8,2,16,128]{4,3,2,1,0:T(8,128)(2,1)S(1)} %select_convert_fusion), channel_id=1, source_target_pairs={{64,0},{128,64},{192,128},{65,1},{129,65},{193,129},{66,2},{130,66... | collective-permute-start | bytes 786440 | tf_op jit(solution)/shard_map/ppermute | solution.py:220
  47.2 9.0 %collective-permute-done.9 = bf16[4,8,2,16,128]{4,3,2,1,0:T(8,128)(2,1)S(1)} collective-permute-done((bf16[4,8,2,16,128]{4,3,2,1,0:T(8,128)(2,1)S(1)}, bf16[4,8,2,16,128]{4,3,2,1,0:T(8,128)(2,1)S(1)}, u32[]{:S(2)}, u32[]{:S(2)}) %collective-permute-start.9) | collective-permute-done | bytes 262176 | tf_op jit(solution)/shard_map/ppermute | solution.py:220
  56.2 0.9 %fusion.7 = bf16[4,8,2,16,128]{4,3,2,1,0:T(8,128)(2,1)} fusion(bf16[4,8,2,16,128]{4,3,2,1,0:T(8,128)(2,1)S(1)} %collective-permute-done.8, bf16[4,8,2,16,128]{4,3,2,1,0:T(8,128)(2,1)S(1)} %collective-permute-done.9, f32[4,8,2,16,128]{4,3,2,1,0:T(8,128)S(1)} %get-tuple-element.17, f32[8,2,16,128]{3,2,1,0:T(8,128)S(1)} %get-tuple-element.19, ...), kind=kLoop, calls=%fused_computation.10 | loop fusion | flops 1310720 | bytes 1441805 | tf_op jit(solution)/shard_map/convert_element_type | solution.py:282
  57.1 8.6 %all-to-all-start.1 = ((bf16[32,2,16,128]{3,2,1,0:T(8,128)(2,1)}), bf16[32,2,16,128]{3,2,1,0:T(8,128)(2,1)S(1)}, u32[]{:S(2)}, u32[]{:S(2)}) async-start(bf16[32,2,16,128]{3,2,1,0:T(8,128)(2,1)} %bitcast.1), calls=%async_computation.1 | async-start | bytes 524288 | tf_op jit(solution)/shard_map/all_to_all | solution.py:224
  65.7 2.7 %copy-done.1 = bf16[10,1152,256]{2,1,0:T(8,128)(2,1)S(1)} copy-done((bf16[10,1152,256]{2,1,0:T(8,128)(2,1)S(1)}, bf16[10,1152,256]{2,1,0:T(8,128)(2,1)}, u32[]{:S(2)}) %copy-start.1) | copy-done | bytes 5898264
  68.4 2.3 %attn_dq.1 = (bf16[128,640]{1,0:T(8,128)(2,1)S(1)}, bf16[128,640]{1,0:T(8,128)(2,1)S(1)}, bf16[128,640]{1,0:T(8,128)(2,1)S(1)}, bf16[128,640]{1,0:T(8,128)(2,1)S(1)}) custom-call(bf16[10,1152,256]{2,1,0:T(8,128)(2,1)S(1)} %copy-done.1, bf16[128,1152]{1,0:T(8,128)(2,1)S(1)} %get-tuple-element.12.kt_ref), custom_call_target="tpu_custom_call" | custom-call | flops 754974720 | bytes 5898240 | tf_op jit(solution)/shard_map/attn_dq/pallas_call | solution.py:172
  70.7 2.5 %collective-permute-start.5 = (bf16[128,640]{1,0:T(8,128)(2,1)S(1)}, bf16[128,640]{1,0:T(8,128)(2,1)S(1)}, u32[]{:S(2)}, u32[]{:S(2)}) collective-permute-start(bf16[128,640]{1,0:T(8,128)(2,1)S(1)} %get-tuple-element.14), channel_id=1, source_target_pairs={{0,3},{1,0},{2,1},{3,2},{4,7},{5,4},{6,5},{7,6},{8,11},{9,8},{10,9... | collective-permute-start | bytes 491528 | tf_op jit(solution)/shard_map/ppermute | solution.py:220
  73.2 0.6 collective-permute-start.6
  73.8 0.6 collective-permute-start.7
  74.3 3.0 %collective-permute-done.5.refs_1_ = bf16[128,640]{1,0:T(8,128)(2,1)S(1)} collective-permute-done((bf16[128,640]{1,0:T(8,128)(2,1)S(1)}, bf16[128,640]{1,0:T(8,128)(2,1)S(1)}, u32[]{:S(2)}, u32[]{:S(2)}) %collective-permute-start.5) | collective-permute-done | bytes 163872 | tf_op jit(solution)/shard_map/ppermute | solution.py:220
  77.4 2.0 %collective-permute-done.6.refs_2_ = bf16[128,640]{1,0:T(8,128)(2,1)S(1)} collective-permute-done((bf16[128,640]{1,0:T(8,128)(2,1)S(1)}, bf16[128,640]{1,0:T(8,128)(2,1)S(1)}, u32[]{:S(2)}, u32[]{:S(2)}) %collective-permute-start.6) | collective-permute-done | bytes 163872 | tf_op jit(solution)/shard_map/ppermute | solution.py:220
  79.4 4.7 %collective-permute-done.7.refs_3_ = bf16[128,640]{1,0:T(8,128)(2,1)S(1)} collective-permute-done((bf16[128,640]{1,0:T(8,128)(2,1)S(1)}, bf16[128,640]{1,0:T(8,128)(2,1)S(1)}, u32[]{:S(2)}, u32[]{:S(2)}) %collective-permute-start.7) | collective-permute-done | bytes 163872 | tf_op jit(solution)/shard_map/ppermute | solution.py:220
  84.1 0.9 %join_heads.1 = bf16[128,2560]{1,0:T(8,128)(2,1)} custom-call(bf16[128,640]{1,0:T(8,128)(2,1)S(1)} %get-tuple-element.13.refs_0_, bf16[128,640]{1,0:T(8,128)(2,1)S(1)} %collective-permute-done.5.refs_1_, bf16[128,640]{1,0:T(8,128)(2,1)S(1)} %collective-permute-done.6.refs_2_, bf16[128,640]{1,0:T(8,128)(2,1)S(1)} %collective-permute-done.7.refs_3_), custom_call_target="tpu_custom_call" | custom-call | tf_op jit(solution)/shard_map/join_heads/pallas_call | solution.py:205
  85.0 0.6 copy_bitcast_fusion
  (23 shorter events, 0.5 us)
Async XLA Ops:
  0.6 18.5 %copy-start.2 = (bf16[2,128,512]{2,1,0:T(8,128)(2,1)S(1)}, bf16[2,128,512]{2,1,0:T(8,128)(2,1)}, u32[]{:S(2)}) copy-start(bf16[2,128,512]{2,1,0:T(8,128)(2,1)} %param.6) | copy-start | bytes 786436
  0.6 18.3 %copy-start.3 = (s32[4096]{0:T(1024)S(1)}, s32[4096]{0:T(1024)}, u32[]{:S(2)}) copy-start(s32[4096]{0:T(1024)} %param.7) | copy-start | bytes 49156
  2.3 26.7 %collective-permute-start.2 = (bf16[2,128,640]{2,1,0:T(8,128)(2,1)S(1)}, bf16[2,128,640]{2,1,0:T(8,128)(2,1)S(1)}, u32[]{:S(2)}, u32[]{:S(2)}) collective-permute-start(bf16[2,128,640]{2,1,0:T(8,128)(2,1)S(1)} %pad_maximum_fusion.3), channel_id=1, source_target_pairs={{0,3},{1,0},{2,1},{3,2},{4,7},{5,4},{6,5},{7,6},{8,11},{9,8},{10,9... | collective-permute-start | bytes 983048 | tf_op jit(solution)/shard_map/ppermute | solution.py:220
  5.7 23.3 %collective-permute-start.1 = (bf16[2,128,640]{2,1,0:T(8,128)(2,1)S(1)}, bf16[2,128,640]{2,1,0:T(8,128)(2,1)S(1)}, u32[]{:S(2)}, u32[]{:S(2)}) collective-permute-start(bf16[2,128,640]{2,1,0:T(8,128)(2,1)S(1)} %pad_maximum_fusion.2), channel_id=1, source_target_pairs={{0,2},{1,3},{2,0},{3,1},{4,6},{5,7},{6,4},{7,5},{8,10},{9,11},{10,... | collective-permute-start | bytes 983048 | tf_op jit(solution)/shard_map/ppermute | solution.py:220
  6.3 22.6 %collective-permute-start = (bf16[2,128,640]{2,1,0:T(8,128)(2,1)S(1)}, bf16[2,128,640]{2,1,0:T(8,128)(2,1)S(1)}, u32[]{:S(2)}, u32[]{:S(2)}) collective-permute-start(bf16[2,128,640]{2,1,0:T(8,128)(2,1)S(1)} %pad_maximum_fusion.1), channel_id=1, source_target_pairs={{0,1},{1,2},{2,3},{3,0},{4,5},{5,6},{6,7},{7,4},{8,9},{9,10},{10,1... | collective-permute-start | bytes 983048 | tf_op jit(solution)/shard_map/ppermute | solution.py:220
  8.0 4.5 %collective-permute-start.3 = (bf16[2,128,128]{2,1,0:T(8,128)(2,1)S(1)}, bf16[2,128,128]{2,1,0:T(8,128)(2,1)S(1)}, u32[]{:S(2)}, u32[]{:S(2)}) collective-permute-start(bf16[2,128,128]{2,1,0:T(8,128)(2,1)S(1)} %select_select_fusion.refs_6_), channel_id=1, source_target_pairs={{0,64},{64,128},{128,192},{1,65},{65,129},{129,193},{2,66},{66,130... | collective-permute-start | bytes 196616 | tf_op jit(solution)/shard_map/ppermute | solution.py:220
  13.3 11.2 %all-to-all-start = ((bf16[4,2,128,128]{3,2,1,0:T(8,128)(2,1)}), bf16[4,2,128,128]{3,2,1,0:T(8,128)(2,1)S(1)}, u32[]{:S(2)}, u32[]{:S(2)}) async-start(bf16[4,2,128,128]{3,2,1,0:T(8,128)(2,1)} %broadcast_select_fusion.1), calls=%async_computation | async-start | bytes 524288 | tf_op jit(solution)/shard_map/all_to_all | solution.py:224
  24.6 5.0 %collective-permute-start.4 = (bf16[4,2,128,128]{3,2,1,0:T(8,128)(2,1)S(1)}, bf16[4,2,128,128]{3,2,1,0:T(8,128)(2,1)S(1)}, u32[]{:S(2)}, u32[]{:S(2)}) collective-permute-start(bf16[4,2,128,128]{3,2,1,0:T(8,128)(2,1)S(1)} %broadcast_select_fusion), channel_id=1, source_target_pairs={{0,8},{8,0},{1,9},{9,1},{2,10},{10,2},{3,11},{11,3},{4,12},{12,4},... | collective-permute-start | bytes 786440 | tf_op jit(solution)/shard_map/ppermute | solution.py:220
  41.7 2.5 %copy-start = (bf16[10,1152,256]{2,1,0:T(8,128)(2,1)}, bf16[10,1152,256]{2,1,0:T(8,128)(2,1)S(1)}, u32[]{:S(2)}) copy-start(bf16[10,1152,256]{2,1,0:T(8,128)(2,1)S(1)} %get-tuple-element.11.ds_ref) | copy-start | bytes 17694724
  44.2 1.6 %collective-permute-start.8 = (bf16[4,8,2,16,128]{4,3,2,1,0:T(8,128)(2,1)S(1)}, bf16[4,8,2,16,128]{4,3,2,1,0:T(8,128)(2,1)S(1)}, u32[]{:S(2)}, u32[]{:S(2)}) collective-permute-start(bf16[4,8,2,16,128]{4,3,2,1,0:T(8,128)(2,1)S(1)} %get-tuple-element.18), channel_id=1, source_target_pairs={{0,8},{8,0},{1,9},{9,1},{2,10},{10,2},{3,11},{11,3},{4,12},{12,4},... | collective-permute-start | bytes 786440 | tf_op jit(solution)/shard_map/ppermute | solution.py:220
  45.9 10.3 %collective-permute-start.9 = (bf16[4,8,2,16,128]{4,3,2,1,0:T(8,128)(2,1)S(1)}, bf16[4,8,2,16,128]{4,3,2,1,0:T(8,128)(2,1)S(1)}, u32[]{:S(2)}, u32[]{:S(2)}) collective-permute-start(bf16[4,8,2,16,128]{4,3,2,1,0:T(8,128)(2,1)S(1)} %select_convert_fusion), channel_id=1, source_target_pairs={{64,0},{128,64},{192,128},{65,1},{129,65},{193,129},{66,2},{130,66... | collective-permute-start | bytes 786440 | tf_op jit(solution)/shard_map/ppermute | solution.py:220
  57.1 27.8 %all-to-all-start.1 = ((bf16[32,2,16,128]{3,2,1,0:T(8,128)(2,1)}), bf16[32,2,16,128]{3,2,1,0:T(8,128)(2,1)S(1)}, u32[]{:S(2)}, u32[]{:S(2)}) async-start(bf16[32,2,16,128]{3,2,1,0:T(8,128)(2,1)} %bitcast.1), calls=%async_computation.1 | async-start | bytes 524288 | tf_op jit(solution)/shard_map/all_to_all | solution.py:224
  65.7 2.7 %copy-start.1 = (bf16[10,1152,256]{2,1,0:T(8,128)(2,1)S(1)}, bf16[10,1152,256]{2,1,0:T(8,128)(2,1)}, u32[]{:S(2)}) copy-start(bf16[10,1152,256]{2,1,0:T(8,128)(2,1)} %copy-done) | copy-start | bytes 17694724
  70.7 6.7 %collective-permute-start.5 = (bf16[128,640]{1,0:T(8,128)(2,1)S(1)}, bf16[128,640]{1,0:T(8,128)(2,1)S(1)}, u32[]{:S(2)}, u32[]{:S(2)}) collective-permute-start(bf16[128,640]{1,0:T(8,128)(2,1)S(1)} %get-tuple-element.14), channel_id=1, source_target_pairs={{0,3},{1,0},{2,1},{3,2},{4,7},{5,4},{6,5},{7,6},{8,11},{9,8},{10,9... | collective-permute-start | bytes 491528 | tf_op jit(solution)/shard_map/ppermute | solution.py:220
  73.2 6.2 %collective-permute-start.6 = (bf16[128,640]{1,0:T(8,128)(2,1)S(1)}, bf16[128,640]{1,0:T(8,128)(2,1)S(1)}, u32[]{:S(2)}, u32[]{:S(2)}) collective-permute-start(bf16[128,640]{1,0:T(8,128)(2,1)S(1)} %get-tuple-element.15), channel_id=1, source_target_pairs={{0,2},{1,3},{2,0},{3,1},{4,6},{5,7},{6,4},{7,5},{8,10},{9,11},{10,... | collective-permute-start | bytes 491528 | tf_op jit(solution)/shard_map/ppermute | solution.py:220
  73.8 10.3 %collective-permute-start.7 = (bf16[128,640]{1,0:T(8,128)(2,1)S(1)}, bf16[128,640]{1,0:T(8,128)(2,1)S(1)}, u32[]{:S(2)}, u32[]{:S(2)}) collective-permute-start(bf16[128,640]{1,0:T(8,128)(2,1)S(1)} %get-tuple-element.16), channel_id=1, source_target_pairs={{0,1},{1,2},{2,3},{3,0},{4,5},{5,6},{6,7},{7,4},{8,9},{9,10},{10,1... | collective-permute-start | bytes 491528 | tf_op jit(solution)/shard_map/ppermute | solution.py:220

commit v4 on v3

--- a/solution.py
+++ b/solution.py
@@ -62,40 +62,64 @@
     def folded(x):
         return x.reshape(chunk // 8, 8, wide)
 
-    def one(p, sc_ref, dp_ref):
-        places = head_places(p, groups)
-        (sa, na), (sb, nb_) = places
-        qq = jnp.concatenate([qd_ref[sa, 0, :, na], qd_ref[sb, 0, :, nb_]], axis=0)
-        dd = jnp.concatenate([qd_ref[sa, 1, :, na], qd_ref[sb, 1, :, nb_]], axis=0)
-        top = jnp.full((8, wide), -3e38, jnp.float32)
-        for c in range(0, nkeys, chunk):
-            s = lax.dot_general(k_ref[c : c + chunk, :], qq, nt, preferred_element_type=jnp.float32)
+    chunks = range(0, nkeys, chunk)
+
+    class Pair:
+        def __init__(self, p, sc_ref, dp_ref):
+            self.p, self.sc_ref, self.dp_ref = p, sc_ref, dp_ref
+            places = head_places(p, groups)
+            self.qq = jnp.concatenate([qd_ref[slot, 0, :, n] for slot, n in places], axis=0)
+            self.dd = jnp.concatenate([qd_ref[slot, 1, :, n] for slot, n in places], axis=0)
+            self.top = jnp.full((8, wide), -3e38, jnp.float32)
+            self.tot = jnp.zeros((8, wide), jnp.float32)
+            self.dl = jnp.zeros((8, wide), jnp.float32)
+
+        def scores(self, c):
+            s = lax.dot_general(k_ref[c : c + chunk, :], self.qq, nt, preferred_element_type=jnp.float32)
             bias = bias_ref[c : c + chunk, :]
             s = s * c2 + jnp.concatenate([bias, bias], axis=1)
-            sc_ref[c : c + chunk, :] = s
-            top = jnp.maximum(top, jnp.max(folded(s), axis=0))
-        top = jnp.max(top, axis=0, keepdims=True)
-        tot = jnp.zeros((8, wide), jnp.float32)
-        dl = jnp.zeros((8, wide), jnp.float32)
-        for c in range(0, nkeys, chunk):
-            dp = lax.dot_general(v_ref[c : c + chunk, :], dd, nt, preferred_element_type=jnp.float32)
-            e = jnp.exp2(sc_ref[c : c + chunk, :] - top)
-            tot = tot + jnp.sum(folded(e), axis=0)
-            dl = dl + jnp.sum(folded(e * dp), axis=0)
-            sc_ref[c : c + chunk, :] = e
-            dp_ref[c : c + chunk, :] = dp
-        rec = 1.0 / jnp.sum(tot, axis=0, keepdims=True)
-        delta = jnp.sum(dl, axis=0, keepdims=True) * rec
-        for c in range(0, nkeys, chunk):
-            prob = (sc_ref[c : c + chunk, :] * rec).astype(jnp.bfloat16)
-            ds = (prob.astype(jnp.float32) * (dp_ref[c : c + chunk, :] - delta)).astype(jnp.bfloat16)
-            ds_ref[p, c : c + chunk, :] = ds
-            dv_ref[c : c + chunk, :] += jnp.dot(prob, dd, preferred_element_type=jnp.float32)
-            dk_ref[c : c + chunk, :] += jnp.dot(ds, qq, preferred_element_type=jnp.float32)
+            self.sc_ref[c : c + chunk, :] = s
+            self.top = jnp.maximum(self.top, jnp.max(folded(s), axis=0))
+
+        def scored(self):
+            self.top = jnp.max(self.top, axis=0, keepdims=True)
+
+        def sums(self, c):
+            dp = lax.dot_general(v_ref[c : c + chunk, :], self.dd, nt, preferred_element_type=jnp.float32)
+            e = jnp.exp2(self.sc_ref[c : c + chunk, :] - self.top)
+            self.tot = self.tot + jnp.sum(folded(e), axis=0)
+            self.dl = self.dl + jnp.sum(folded(e * dp), axis=0)
+            self.sc_ref[c : c + chunk, :] = e
+            self.dp_ref[c : c + chunk, :] = dp
+
+        def summed(self):
+            self.rec = 1.0 / jnp.sum(self.tot, axis=0, keepdims=True)
+            self.delta = jnp.sum(self.dl, axis=0, keepdims=True) * self.rec
+
+        def grads(self, c):
+            prob = (self.sc_ref[c : c + chunk, :] * self.rec).astype(jnp.bfloat16)
+            ds = prob.astype(jnp.float32) * (self.dp_ref[c : c + chunk, :] - self.delta)
+            ds = ds.astype(jnp.bfloat16)
+            ds_ref[self.p, c : c + chunk, :] = ds
+            dv_ref[c : c + chunk, :] += jnp.dot(prob, self.dd, preferred_element_type=jnp.float32)
+            dk_ref[c : c + chunk, :] += jnp.dot(ds, self.qq, preferred_element_type=jnp.float32)
 
     def step(t, carry):
-        for u in range(2):
-            one(2 * t + u, pairs[2 * u], pairs[2 * u + 1])
+        one, two = [Pair(2 * t + u, *pairs[2 * u : 2 * u + 2]) for u in (0, 1)]
+        for c in chunks:
+            one.scores(c)
+        one.scored()
+        for c in chunks:
+            one.sums(c)
+            two.scores(c)
+        one.summed()
+        two.scored()
+        for c in chunks:
+            one.grads(c)
+            two.sums(c)
+        two.summed()
+        for c in chunks:
+            two.grads(c)
         return carry
 
     lax.fori_loop(0, slots * groups // 4, step, 0)
@@ -245,14 +269,13 @@
         at = lax.rem(head + k, ring) * part
         return jnp.stack([lax.dynamic_slice_in_dim(a[0], at, part, 1) for a in arrays])
 
-    far = cut((queries, grad_out), 2)
-    pieces = {2: shifted(far, "x", 2, True)}
+    pieces = lax.optimization_barrier([cut((queries, grad_out), k) for k in range(ring)])
     own = chosen(head, jnp.split(keys_values, ring, axis=2))
+    own = lax.optimization_barrier((own, pieces[1]))[0]
     prev = shifted(own, "y", 1, False)
-    near = (queries, grad_out)
+    pieces[2] = shifted(pieces[2], "x", 2, True)
     for k in (1, 3):
-        pieces[k] = shifted(cut(near, k), "x", k, True)
-    pieces = [cut(near, 0), pieces[1], pieces[2], pieces[3]]
+        pieces[k] = shifted(pieces[k], "x", k, True)
     line = exchanged(jnp.where(chips > chip, own[None], prev[None]), "z")
     cross = jnp.where(chips == chip, jnp.where(core == 1, prev, own)[None], line)
     cross = shifted(cross, "core", 1, True)

time: 86 us -> 82.5 us (0.959)
  waiting for transfers between devices: 27.3 us -> 25 us
  Pallas kernels: 15.1 us -> 13.8 us
    ppermute x10, waiting for transfers between devices: 21.9 us -> 19.5 us  [shifted(): return lax.ppermute(value, axis, pairs)]
    ppermute x10, starting transfers between devices: 17.1 us -> 18.8 us  [shifted(): return lax.ppermute(value, axis, pairs)]
    all_to_all x2, starting transfers between devices: 14.2 us -> 12.7 us  [exchanged(): return lax.all_to_all(value, axes, 0, 0, tiled=True)]
    pallas_call x1, Pallas kernels: 12 us -> 10.6 us  [attn_parts(): pl.pallas_call(functools.partial(attn_kernel, slots, chunk), out_shape=(j...]
    unnamed x8 -> x6, local copies, waits for them, and re-layouts: 5.21 us -> 5.19 us
  transfers between devices with their start and end apart: 12 -> 12, of which waited for: 8 -> 7; matrix products, arithmetic and copies ran while one was open for 3% -> 3% of each run, Pallas kernels for 4% -> 4%
where the time goes in v4:
time: 82.5 us; the launch traced here: 82.1 us
  starting transfers between devices  31.4 us (38%)
  waiting for transfers between devices  25 us (30%)
  Pallas kernels  13.8 us (17%)
  local copies, waits for them, and re-layouts  7.4 us (9%)
  other arithmetic  3.59 us (4%)
  between operations  0.85 us (1%)
    ppermute x10, waiting for transfers between devices, shifted(): return lax.ppermute(value, axis, pairs)  19.5 us
    ppermute x10, starting transfers between devices, shifted(): return lax.ppermute(value, axis, pairs)  18.8 us
    all_to_all x2, starting transfers between devices, exchanged(): return lax.all_to_all(value, axes, 0, 0, tiled=True)  12.7 us
    pallas_call x1, Pallas kernels, attn_parts(): pl.pallas_call(functools.partial(attn_kernel, slots, chunk), out_shape=(j...  10.6 us
    all_to_all x2, waiting for transfers between devices, exchanged(): return lax.all_to_all(value, axes, 0, 0, tiled=True)  5.5 us
    unnamed x6, local copies, waits for them, and re-layouts  5.19 us
    pallas_call x1, Pallas kernels, dq_parts(): pl.pallas_call(functools.partial(dq_kernel, slots), out_shape=tuple((jax....  2.31 us
  transfers between devices with their start and end apart: 12, of which 7 were waited for; matrix products, arithmetic and copies ran while one was open for 3% of the time, Pallas kernels for 4%

profile of v4, /device:TPU:1, one launch (start us, length us, event | category | flops | bytes accessed | tf_op | source)
XLA Modules:
  0.0 82.1 jit_solution(1677070642575669140)
XLA Ops:
  0.7 1.5 %constant_dynamic-slice_fusion = (bf16[1,128,640]{2,1,0:T(8,128)(2,1)S(1)}, bf16[1,128,640]{2,1,0:T(8,128)(2,1)S(1)}, bf16[1,128,640]{2,1,0:T(8,128)(2,1)S(1)}, ...) fusion(bf16[1,128,2560]{2,1,0:T(8,128)(2,1)} %param.5, ...), kind=kLoop, calls=%fused_computation.23 | loop fusion | bytes 2621456 | tf_op jit(solution)/shard_map/dynamic_slice | solution.py:270
  2.4 2.1 %collective-permute-start = (bf16[2,128,640]{2,1,0:T(8,128)(2,1)S(1)}, bf16[2,128,640]{2,1,0:T(8,128)(2,1)S(1)}, u32[]{:S(2)}, u32[]{:S(2)}) collective-permute-start(bf16[2,128,640]{2,1,0:T(8,128)(2,1)S(1)} %pad_maximum_fusion.1), channel_id=1, source_target_pairs={{0,1},{1,2},{2,3},{3,0},{4,5},{5,6},{6,7},{7,4},{8,9},{9,10},{10,1... | collective-permute-start | bytes 983048 | tf_op jit(solution)/shard_map/ppermute | solution.py:244
  4.5 1.0 %select_select_fusion.refs_6_ = bf16[2,128,128]{2,1,0:T(8,128)(2,1)S(1)} fusion(bf16[2,128,512]{2,1,0:T(8,128)(2,1)} %param.6, pred[]{:T(512)S(6)} %eq.45, pred[]{:T(512)S(6)} %eq.44, pred[]{:T(512)S(6)} %eq.43), kind=kLoop, calls=%fused_computation.18 | loop fusion | flops 98304 | bytes 327683 | tf_op jit(solution)/shard_map/jit(_where)/select_n | solution.py:254
  5.4 3.2 %collective-permute-start.3 = (bf16[2,128,128]{2,1,0:T(8,128)(2,1)S(1)}, bf16[2,128,128]{2,1,0:T(8,128)(2,1)S(1)}, u32[]{:S(2)}, u32[]{:S(2)}) collective-permute-start(bf16[2,128,128]{2,1,0:T(8,128)(2,1)S(1)} %select_select_fusion.refs_6_), channel_id=1, source_target_pairs={{0,64},{64,128},{128,192},{1,65},{65,129},{129,193},{2,66},{66,130... | collective-permute-start | bytes 196616 | tf_op jit(solution)/shard_map/ppermute | solution.py:244
  8.7 2.5 %collective-permute-start.1 = (bf16[2,128,640]{2,1,0:T(8,128)(2,1)S(1)}, bf16[2,128,640]{2,1,0:T(8,128)(2,1)S(1)}, u32[]{:S(2)}, u32[]{:S(2)}) collective-permute-start(bf16[2,128,640]{2,1,0:T(8,128)(2,1)S(1)} %pad_maximum_fusion.2), channel_id=1, source_target_pairs={{0,2},{1,3},{2,0},{3,1},{4,6},{5,7},{6,4},{7,5},{8,10},{9,11},{10,... | collective-permute-start | bytes 983048 | tf_op jit(solution)/shard_map/ppermute | solution.py:244
  11.2 1.2 %collective-permute-start.2 = (bf16[2,128,640]{2,1,0:T(8,128)(2,1)S(1)}, bf16[2,128,640]{2,1,0:T(8,128)(2,1)S(1)}, u32[]{:S(2)}, u32[]{:S(2)}) collective-permute-start(bf16[2,128,640]{2,1,0:T(8,128)(2,1)S(1)} %pad_maximum_fusion.3), channel_id=1, source_target_pairs={{0,3},{1,0},{2,1},{3,2},{4,7},{5,4},{6,5},{7,6},{8,11},{9,8},{10,9... | collective-permute-start | bytes 983048 | tf_op jit(solution)/shard_map/ppermute | solution.py:244
  12.4 0.8 broadcast_select_fusion.1
  13.2 5.6 %all-to-all-start = ((bf16[4,2,128,128]{3,2,1,0:T(8,128)(2,1)}), bf16[4,2,128,128]{3,2,1,0:T(8,128)(2,1)S(1)}, u32[]{:S(2)}, u32[]{:S(2)}) async-start(bf16[4,2,128,128]{3,2,1,0:T(8,128)(2,1)} %broadcast_select_fusion.1), calls=%async_computation | async-start | bytes 524288 | tf_op jit(solution)/shard_map/all_to_all | solution.py:248
  18.9 5.5 %all-to-all-done.refs_4_ = bf16[4,2,128,128]{3,2,1,0:T(8,128)(2,1)S(1)} async-done(((bf16[4,2,128,128]{3,2,1,0:T(8,128)(2,1)}), bf16[4,2,128,128]{3,2,1,0:T(8,128)(2,1)S(1)}, u32[]{:S(2)}, u32[]{:S(2)}) %all-to-all-start) | async-done | bytes 262176 | tf_op jit(solution)/shard_map/all_to_all | solution.py:248
  24.4 0.1 broadcast_select_fusion
  24.5 4.4 %collective-permute-start.4 = (bf16[4,2,128,128]{3,2,1,0:T(8,128)(2,1)S(1)}, bf16[4,2,128,128]{3,2,1,0:T(8,128)(2,1)S(1)}, u32[]{:S(2)}, u32[]{:S(2)}) collective-permute-start(bf16[4,2,128,128]{3,2,1,0:T(8,128)(2,1)S(1)} %broadcast_select_fusion), channel_id=1, source_target_pairs={{0,8},{8,0},{1,9},{9,1},{2,10},{10,2},{3,11},{11,3},{4,12},{12,4},... | collective-permute-start | bytes 786440 | tf_op jit(solution)/shard_map/ppermute | solution.py:244
  29.0 0.4 fusion.1.refs_8_
  29.4 0.8 collective-permute-done.4.refs_7_
  30.1 10.6 %attn_bwd.1 = (bf16[10,1152,256]{2,1,0:T(8,128)(2,1)S(1)}, bf16[128,1152]{1,0:T(8,128)(2,1)S(1)}, f32[4,8,2,16,128]{4,3,2,1,0:T(8,128)S(1)}, f32[8,2,16,128]{3,2...) custom-call(bf16[2,128,640]{2,1,0:T(8,128)(2,1)S(1)} %pad_maximum_fusion.refs_0_, ...), custom_call_target="tpu_custom_call" | custom-call | flops 3019898880 | bytes 4194304 | tf_op jit(solution)/shard_map/attn_bwd/pallas_call | solution.py:145
  40.7 2.5 %copy-done = bf16[10,1152,256]{2,1,0:T(8,128)(2,1)} copy-done((bf16[10,1152,256]{2,1,0:T(8,128)(2,1)}, bf16[10,1152,256]{2,1,0:T(8,128)(2,1)S(1)}, u32[]{:S(2)}) %copy-start) | copy-done | bytes 5898264
  43.3 0.4 collective-permute-start.8
  43.6 1.2 %collective-permute-done.8 = bf16[4,8,2,16,128]{4,3,2,1,0:T(8,128)(2,1)S(1)} collective-permute-done((bf16[4,8,2,16,128]{4,3,2,1,0:T(8,128)(2,1)S(1)}, bf16[4,8,2,16,128]{4,3,2,1,0:T(8,128)(2,1)S(1)}, u32[]{:S(2)}, u32[]{:S(2)}) %collective-permute-start.8) | collective-permute-done | bytes 262176 | tf_op jit(solution)/shard_map/ppermute | solution.py:244
  44.8 0.2 select_convert_fusion
  44.9 1.3 %collective-permute-start.9 = (bf16[4,8,2,16,128]{4,3,2,1,0:T(8,128)(2,1)S(1)}, bf16[4,8,2,16,128]{4,3,2,1,0:T(8,128)(2,1)S(1)}, u32[]{:S(2)}, u32[]{:S(2)}) collective-permute-start(bf16[4,8,2,16,128]{4,3,2,1,0:T(8,128)(2,1)S(1)} %select_convert_fusion), channel_id=1, source_target_pairs={{64,0},{128,64},{192,128},{65,1},{129,65},{193,129},{66,2},{130,66... | collective-permute-start | bytes 786440 | tf_op jit(solution)/shard_map/ppermute | solution.py:244
  46.3 8.1 %collective-permute-done.9 = bf16[4,8,2,16,128]{4,3,2,1,0:T(8,128)(2,1)S(1)} collective-permute-done((bf16[4,8,2,16,128]{4,3,2,1,0:T(8,128)(2,1)S(1)}, bf16[4,8,2,16,128]{4,3,2,1,0:T(8,128)(2,1)S(1)}, u32[]{:S(2)}, u32[]{:S(2)}) %collective-permute-start.9) | collective-permute-done | bytes 262176 | tf_op jit(solution)/shard_map/ppermute | solution.py:244
  54.3 0.9 %fusion.7 = bf16[4,8,2,16,128]{4,3,2,1,0:T(8,128)(2,1)} fusion(bf16[4,8,2,16,128]{4,3,2,1,0:T(8,128)(2,1)S(1)} %collective-permute-done.8, bf16[4,8,2,16,128]{4,3,2,1,0:T(8,128)(2,1)S(1)} %collective-permute-done.9, f32[4,8,2,16,128]{4,3,2,1,0:T(8,128)S(1)} %get-tuple-element.27, f32[8,2,16,128]{3,2,1,0:T(8,128)S(1)} %get-tuple-element.29, ...), kind=kLoop, calls=%fused_computation.10 | loop fusion | flops 1310720 | bytes 1441805 | tf_op jit(solution)/shard_map/convert_element_type | solution.py:305
  55.3 7.0 %all-to-all-start.1 = ((bf16[32,2,16,128]{3,2,1,0:T(8,128)(2,1)}), bf16[32,2,16,128]{3,2,1,0:T(8,128)(2,1)S(1)}, u32[]{:S(2)}, u32[]{:S(2)}) async-start(bf16[32,2,16,128]{3,2,1,0:T(8,128)(2,1)} %bitcast.1), calls=%async_computation.1 | async-start | bytes 524288 | tf_op jit(solution)/shard_map/all_to_all | solution.py:248
  62.3 2.7 %copy-done.1 = bf16[10,1152,256]{2,1,0:T(8,128)(2,1)S(1)} copy-done((bf16[10,1152,256]{2,1,0:T(8,128)(2,1)S(1)}, bf16[10,1152,256]{2,1,0:T(8,128)(2,1)}, u32[]{:S(2)}) %copy-start.1) | copy-done | bytes 5898264
  65.0 2.3 %attn_dq.1 = (bf16[128,640]{1,0:T(8,128)(2,1)S(1)}, bf16[128,640]{1,0:T(8,128)(2,1)S(1)}, bf16[128,640]{1,0:T(8,128)(2,1)S(1)}, bf16[128,640]{1,0:T(8,128)(2,1)S(1)}) custom-call(bf16[10,1152,256]{2,1,0:T(8,128)(2,1)S(1)} %copy-done.1, bf16[128,1152]{1,0:T(8,128)(2,1)S(1)} %get-tuple-element.22.kt_ref), custom_call_target="tpu_custom_call" | custom-call | flops 754974720 | bytes 5898240 | tf_op jit(solution)/shard_map/attn_dq/pallas_call | solution.py:196
  67.3 2.5 %collective-permute-start.5 = (bf16[128,640]{1,0:T(8,128)(2,1)S(1)}, bf16[128,640]{1,0:T(8,128)(2,1)S(1)}, u32[]{:S(2)}, u32[]{:S(2)}) collective-permute-start(bf16[128,640]{1,0:T(8,128)(2,1)S(1)} %get-tuple-element.24), channel_id=1, source_target_pairs={{0,3},{1,0},{2,1},{3,2},{4,7},{5,4},{6,5},{7,6},{8,11},{9,8},{10,9... | collective-permute-start | bytes 491528 | tf_op jit(solution)/shard_map/ppermute | solution.py:244
  69.8 0.6 collective-permute-start.6
  70.4 0.6 collective-permute-start.7
  71.0 2.7 %collective-permute-done.5.refs_1_ = bf16[128,640]{1,0:T(8,128)(2,1)S(1)} collective-permute-done((bf16[128,640]{1,0:T(8,128)(2,1)S(1)}, bf16[128,640]{1,0:T(8,128)(2,1)S(1)}, u32[]{:S(2)}, u32[]{:S(2)}) %collective-permute-start.5) | collective-permute-done | bytes 163872 | tf_op jit(solution)/shard_map/ppermute | solution.py:244
  73.7 2.3 %collective-permute-done.6.refs_2_ = bf16[128,640]{1,0:T(8,128)(2,1)S(1)} collective-permute-done((bf16[128,640]{1,0:T(8,128)(2,1)S(1)}, bf16[128,640]{1,0:T(8,128)(2,1)S(1)}, u32[]{:S(2)}, u32[]{:S(2)}) %collective-permute-start.6) | collective-permute-done | bytes 163872 | tf_op jit(solution)/shard_map/ppermute | solution.py:244
  75.9 4.6 %collective-permute-done.7.refs_3_ = bf16[128,640]{1,0:T(8,128)(2,1)S(1)} collective-permute-done((bf16[128,640]{1,0:T(8,128)(2,1)S(1)}, bf16[128,640]{1,0:T(8,128)(2,1)S(1)}, u32[]{:S(2)}, u32[]{:S(2)}) %collective-permute-start.7) | collective-permute-done | bytes 163872 | tf_op jit(solution)/shard_map/ppermute | solution.py:244
  80.5 0.9 %join_heads.1 = bf16[128,2560]{1,0:T(8,128)(2,1)} custom-call(bf16[128,640]{1,0:T(8,128)(2,1)S(1)} %get-tuple-element.23.refs_0_, bf16[128,640]{1,0:T(8,128)(2,1)S(1)} %collective-permute-done.5.refs_1_, bf16[128,640]{1,0:T(8,128)(2,1)S(1)} %collective-permute-done.6.refs_2_, bf16[128,640]{1,0:T(8,128)(2,1)S(1)} %collective-permute-done.7.refs_3_), custom_call_target="tpu_custom_call" | custom-call | tf_op jit(solution)/shard_map/join_heads/pallas_call | solution.py:229
  81.4 0.6 copy_bitcast_fusion
  (21 shorter events, 0.4 us)
Async XLA Ops:
  0.6 18.1 %copy-start.2 = (s32[4096]{0:T(1024)S(1)}, s32[4096]{0:T(1024)}, u32[]{:S(2)}) copy-start(s32[4096]{0:T(1024)} %param.7) | copy-start | bytes 49156
  2.4 27.0 %collective-permute-start = (bf16[2,128,640]{2,1,0:T(8,128)(2,1)S(1)}, bf16[2,128,640]{2,1,0:T(8,128)(2,1)S(1)}, u32[]{:S(2)}, u32[]{:S(2)}) collective-permute-start(bf16[2,128,640]{2,1,0:T(8,128)(2,1)S(1)} %pad_maximum_fusion.1), channel_id=1, source_target_pairs={{0,1},{1,2},{2,3},{3,0},{4,5},{5,6},{6,7},{7,4},{8,9},{9,10},{10,1... | collective-permute-start | bytes 983048 | tf_op jit(solution)/shard_map/ppermute | solution.py:244
  5.4 6.9 %collective-permute-start.3 = (bf16[2,128,128]{2,1,0:T(8,128)(2,1)S(1)}, bf16[2,128,128]{2,1,0:T(8,128)(2,1)S(1)}, u32[]{:S(2)}, u32[]{:S(2)}) collective-permute-start(bf16[2,128,128]{2,1,0:T(8,128)(2,1)S(1)} %select_select_fusion.refs_6_), channel_id=1, source_target_pairs={{0,64},{64,128},{128,192},{1,65},{65,129},{129,193},{2,66},{66,130... | collective-permute-start | bytes 196616 | tf_op jit(solution)/shard_map/ppermute | solution.py:244
  8.7 20.7 %collective-permute-start.1 = (bf16[2,128,640]{2,1,0:T(8,128)(2,1)S(1)}, bf16[2,128,640]{2,1,0:T(8,128)(2,1)S(1)}, u32[]{:S(2)}, u32[]{:S(2)}) collective-permute-start(bf16[2,128,640]{2,1,0:T(8,128)(2,1)S(1)} %pad_maximum_fusion.2), channel_id=1, source_target_pairs={{0,2},{1,3},{2,0},{3,1},{4,6},{5,7},{6,4},{7,5},{8,10},{9,11},{10,... | collective-permute-start | bytes 983048 | tf_op jit(solution)/shard_map/ppermute | solution.py:244
  11.2 18.2 %collective-permute-start.2 = (bf16[2,128,640]{2,1,0:T(8,128)(2,1)S(1)}, bf16[2,128,640]{2,1,0:T(8,128)(2,1)S(1)}, u32[]{:S(2)}, u32[]{:S(2)}) collective-permute-start(bf16[2,128,640]{2,1,0:T(8,128)(2,1)S(1)} %pad_maximum_fusion.3), channel_id=1, source_target_pairs={{0,3},{1,0},{2,1},{3,2},{4,7},{5,4},{6,5},{7,6},{8,11},{9,8},{10,9... | collective-permute-start | bytes 983048 | tf_op jit(solution)/shard_map/ppermute | solution.py:244
  13.2 11.3 %all-to-all-start = ((bf16[4,2,128,128]{3,2,1,0:T(8,128)(2,1)}), bf16[4,2,128,128]{3,2,1,0:T(8,128)(2,1)S(1)}, u32[]{:S(2)}, u32[]{:S(2)}) async-start(bf16[4,2,128,128]{3,2,1,0:T(8,128)(2,1)} %broadcast_select_fusion.1), calls=%async_computation | async-start | bytes 524288 | tf_op jit(solution)/shard_map/all_to_all | solution.py:248
  24.5 5.6 %collective-permute-start.4 = (bf16[4,2,128,128]{3,2,1,0:T(8,128)(2,1)S(1)}, bf16[4,2,128,128]{3,2,1,0:T(8,128)(2,1)S(1)}, u32[]{:S(2)}, u32[]{:S(2)}) collective-permute-start(bf16[4,2,128,128]{3,2,1,0:T(8,128)(2,1)S(1)} %broadcast_select_fusion), channel_id=1, source_target_pairs={{0,8},{8,0},{1,9},{9,1},{2,10},{10,2},{3,11},{11,3},{4,12},{12,4},... | collective-permute-start | bytes 786440 | tf_op jit(solution)/shard_map/ppermute | solution.py:244
  40.7 2.5 %copy-start = (bf16[10,1152,256]{2,1,0:T(8,128)(2,1)}, bf16[10,1152,256]{2,1,0:T(8,128)(2,1)S(1)}, u32[]{:S(2)}) copy-start(bf16[10,1152,256]{2,1,0:T(8,128)(2,1)S(1)} %get-tuple-element.21.ds_ref) | copy-start | bytes 17694724
  43.3 1.5 %collective-permute-start.8 = (bf16[4,8,2,16,128]{4,3,2,1,0:T(8,128)(2,1)S(1)}, bf16[4,8,2,16,128]{4,3,2,1,0:T(8,128)(2,1)S(1)}, u32[]{:S(2)}, u32[]{:S(2)}) collective-permute-start(bf16[4,8,2,16,128]{4,3,2,1,0:T(8,128)(2,1)S(1)} %get-tuple-element.28), channel_id=1, source_target_pairs={{0,8},{8,0},{1,9},{9,1},{2,10},{10,2},{3,11},{11,3},{4,12},{12,4},... | collective-permute-start | bytes 786440 | tf_op jit(solution)/shard_map/ppermute | solution.py:244
  44.9 9.4 %collective-permute-start.9 = (bf16[4,8,2,16,128]{4,3,2,1,0:T(8,128)(2,1)S(1)}, bf16[4,8,2,16,128]{4,3,2,1,0:T(8,128)(2,1)S(1)}, u32[]{:S(2)}, u32[]{:S(2)}) collective-permute-start(bf16[4,8,2,16,128]{4,3,2,1,0:T(8,128)(2,1)S(1)} %select_convert_fusion), channel_id=1, source_target_pairs={{64,0},{128,64},{192,128},{65,1},{129,65},{193,129},{66,2},{130,66... | collective-permute-start | bytes 786440 | tf_op jit(solution)/shard_map/ppermute | solution.py:244
  55.3 26.1 %all-to-all-start.1 = ((bf16[32,2,16,128]{3,2,1,0:T(8,128)(2,1)}), bf16[32,2,16,128]{3,2,1,0:T(8,128)(2,1)S(1)}, u32[]{:S(2)}, u32[]{:S(2)}) async-start(bf16[32,2,16,128]{3,2,1,0:T(8,128)(2,1)} %bitcast.1), calls=%async_computation.1 | async-start | bytes 524288 | tf_op jit(solution)/shard_map/all_to_all | solution.py:248
  62.3 2.7 %copy-start.1 = (bf16[10,1152,256]{2,1,0:T(8,128)(2,1)S(1)}, bf16[10,1152,256]{2,1,0:T(8,128)(2,1)}, u32[]{:S(2)}) copy-start(bf16[10,1152,256]{2,1,0:T(8,128)(2,1)} %copy-done) | copy-start | bytes 17694724
  67.3 6.4 %collective-permute-start.5 = (bf16[128,640]{1,0:T(8,128)(2,1)S(1)}, bf16[128,640]{1,0:T(8,128)(2,1)S(1)}, u32[]{:S(2)}, u32[]{:S(2)}) collective-permute-start(bf16[128,640]{1,0:T(8,128)(2,1)S(1)} %get-tuple-element.24), channel_id=1, source_target_pairs={{0,3},{1,0},{2,1},{3,2},{4,7},{5,4},{6,5},{7,6},{8,11},{9,8},{10,9... | collective-permute-start | bytes 491528 | tf_op jit(solution)/shard_map/ppermute | solution.py:244
  69.8 6.1 %collective-permute-start.6 = (bf16[128,640]{1,0:T(8,128)(2,1)S(1)}, bf16[128,640]{1,0:T(8,128)(2,1)S(1)}, u32[]{:S(2)}, u32[]{:S(2)}) collective-permute-start(bf16[128,640]{1,0:T(8,128)(2,1)S(1)} %get-tuple-element.25), channel_id=1, source_target_pairs={{0,2},{1,3},{2,0},{3,1},{4,6},{5,7},{6,4},{7,5},{8,10},{9,11},{10,... | collective-permute-start | bytes 491528 | tf_op jit(solution)/shard_map/ppermute | solution.py:244
  70.4 10.1 %collective-permute-start.7 = (bf16[128,640]{1,0:T(8,128)(2,1)S(1)}, bf16[128,640]{1,0:T(8,128)(2,1)S(1)}, u32[]{:S(2)}, u32[]{:S(2)}) collective-permute-start(bf16[128,640]{1,0:T(8,128)(2,1)S(1)} %get-tuple-element.26), channel_id=1, source_target_pairs={{0,1},{1,2},{2,3},{3,0},{4,5},{5,6},{6,7},{7,4},{8,9},{9,10},{10,1... | collective-permute-start | bytes 491528 | tf_op jit(solution)/shard_map/ppermute | solution.py:244
